TPU v7x, 32 devices: a whole 2x2x4 slice. The times are simulated.
32 devices in a mesh: groups: 2 (over x), hist: 8 (over z, y), users: 2 (over core).
Axes of the slice: x: 2, y: 2, z: 4, core: 2. Of those that a mesh axis runs over, the one named last changes fastest.
Arguments:
- targets: bfloat16 [4, 512, 1024], P(('groups', 'users'), 'hist'), parts along dimension 0, may hold values from -6 to 6
- hist_keys: bfloat16 [2, 4, 12288, 1024], P(None, ('groups', 'users'), 'hist'), parts along dimension 1, may hold values from -6 to 6
- hist_values: bfloat16 [2, 4, 12288, 1024], P(None, ('groups', 'users'), 'hist'), parts along dimension 1, may hold values from -6 to 6
- lengths: int32 [4], P(('groups', 'users')), parts along dimension 0, may hold values from 3072 to 12288
- cuts: int32 [4, 512], P(('groups', 'users')), parts along dimension 0, may hold values from 1 to 12288
- w_query: bfloat16 [2, 1024, 1024], replicated, may hold values from -0.1875 to 0.1875
- w_gate: bfloat16 [2, 1024, 1024], replicated, may hold values from -0.1875 to 0.1875
- w_out: bfloat16 [2, 1024, 1024], replicated, may hold values from -0.1875 to 0.1875
- ln_gain: float32 [2, 1024], replicated, may hold values from 0.1 to 1.9
Outputs:
- refined: bfloat16 [4, 512, 1024], P(('groups', 'users'), 'hist'), parts along dimension 0
There are 2 independent parts, one for each index of `groups`. A program takes and returns all parts, laid end to end along the dimension named above; an argument that names none is the same for every part. Nothing has to cross between parts.
All inputs are finite; a program needn't handle non-finite values.
Results may differ from a plain program's by a relative error of at most 0.012.
Values may be sent and summed in bfloat16 or wider, within the bound.
No kernel may reach another device: no remote copies, remote signals or barrier semaphores. Data moves between devices by JAX's collectives and lax.ppermute only.
A program may use at most 128 MiB of HBM per device.

v0:
```python
import functools
import math

import jax
import jax.numpy as jnp
from jax import lax
from jax.experimental import pallas as pl
from jax.experimental.pallas import tpu as pltpu
from jax.sharding import PartitionSpec as P

HEADS = 8
CHUNKS = 2
ROW_TILE = 256
HIST_TILE = 512
STEP_HEADS = 2
LIMITS_COST = 20
ATTEND_VMEM = 16 * 2**20
FINISH_VMEM = 16 * 2**20


def limits_kernel(size, deep, step_long, hist_rows, length_ref, cuts_ref, *refs):
    outs, by_row = refs[:-1], refs[-1]
    me = lax.axis_index("hist")
    limit = jnp.minimum(cuts_ref[...], length_ref[0]) - me * hist_rows
    by_row[...] = jnp.broadcast_to(limit, (by_row.shape[1], limit.shape[1])).T
    own_rows = by_row.shape[0] // size
    z, y = me // deep, me % deep
    for across, out in enumerate(outs):
        for step in range(size // deep):
            owner = step_long(z, step) * deep + (y ^ across)
            rows = pl.ds(pl.multiple_of(owner * own_rows, own_rows), own_rows)
            out[step * own_rows : (step + 1) * own_rows, :] = by_row[rows, :]


def row_limits(size, deep, step_long, hist_rows, lengths, cuts):
    rows = cuts.shape[1]
    out = jax.ShapeDtypeStruct((rows // deep, 128), jnp.int32)
    return pl.pallas_call(
        functools.partial(limits_kernel, size, deep, step_long, hist_rows),
        in_specs=[
            pl.BlockSpec(memory_space=pltpu.SMEM),
            pl.BlockSpec(memory_space=pltpu.VMEM),
        ],
        out_shape=[out] * deep,
        scratch_shapes=[pltpu.VMEM((rows, 128), jnp.int32)],
        cost_estimate=pl.CostEstimate(
            flops=LIMITS_COST * 10**9, bytes_accessed=LIMITS_COST * 2 * 10**6, transcendentals=0
        ),
        compiler_params=pltpu.CompilerParams(vmem_limit_bytes=4 * 2**20),
    )(lengths, cuts)


def attend_kernel(dim, q_ref, lim_ref, k_ref, v_ref, out_ref):
    rows, width = q_ref.shape
    hist_rows = k_ref.shape[2]
    tile_rows = math.gcd(ROW_TILE, rows)
    tile_hist = math.gcd(HIST_TILE, hist_rows)
    lane = lax.broadcasted_iota(jnp.int32, (tile_rows, tile_hist), 1)
    for c in range(0, width, dim):
        head = slice(c, c + dim)
        for r in range(0, rows, tile_rows):
            q = q_ref[r : r + tile_rows, head]
            lim = lim_ref[r : r + tile_rows, :1]

            def score(j):
                k = k_ref[0, 0, j : j + tile_hist, head]
                return lax.dot_general(
                    q, k, (((1,), (1,)), ((), ())), preferred_element_type=jnp.float32
                )

            acc = None
            ahead = score(0)
            for j in range(0, hist_rows, tile_hist):
                h = ahead
                if j + tile_hist < hist_rows:
                    ahead = score(j + tile_hist)
                w = h * jnp.tanh(h) + h
                w = jnp.where(lane < lim - j, w, 0.0).astype(jnp.bfloat16)
                v = v_ref[0, 0, j : j + tile_hist, head]
                part = jnp.dot(w, v, preferred_element_type=jnp.float32)
                acc = part if acc is None else acc + part
            out_ref[r : r + tile_rows, head] = acc.astype(out_ref.dtype)


def attend(q, lim, keys, values, layer, first_head, dim, out_type):
    rows, width = q.shape
    hist_rows = keys.shape[2]
    step = STEP_HEADS * dim
    first = first_head // STEP_HEADS
    slab = pl.BlockSpec((1, 1, hist_rows, step), lambda h: (layer, 0, 0, first + h))
    return pl.pallas_call(
        functools.partial(attend_kernel, dim),
        grid=(width // step,),
        in_specs=[
            pl.BlockSpec((rows, step), lambda h: (0, h)),
            pl.BlockSpec(lim.shape, lambda h: (0, 0)),
            slab,
            slab,
        ],
        out_specs=pl.BlockSpec((rows, step), lambda h: (0, h)),
        out_shape=jax.ShapeDtypeStruct((rows, width), out_type),
        cost_estimate=pl.CostEstimate(
            flops=4 * rows * hist_rows * width,
            bytes_accessed=4 * hist_rows * width + 4 * rows * width,
            transcendentals=rows * hist_rows * width // dim,
        ),
        compiler_params=pltpu.CompilerParams(
            dimension_semantics=("arbitrary",), vmem_limit_bytes=ATTEND_VMEM
        ),
    )(q, lim, keys, values)


def finish_kernel(half_factor, layer, counts, hidden_ref, gate_ref, gain_ref, out_w_ref, query_w_ref, *refs):
    terms, outs = refs[: sum(counts)], refs[sum(counts) :]
    parts, first = [], 0
    for count in counts:
        total = terms[first][...].astype(jnp.float32)
        for term in terms[first + 1 : first + count]:
            total = total + term[...].astype(jnp.float32)
        parts.append(total)
        first += count
    summed = jnp.concatenate(parts, axis=1)
    centred = summed - jnp.mean(summed, axis=-1, keepdims=True)
    spread = jnp.mean(centred * centred, axis=-1, keepdims=True)
    normed = (centred * lax.rsqrt(spread + 1e-05) * gain_ref[...] * gate_ref[...]).astype(
        jnp.bfloat16
    )
    update = jnp.dot(normed, out_w_ref[layer], preferred_element_type=jnp.float32)
    hidden = (hidden_ref[...].astype(jnp.float32) + update).astype(jnp.bfloat16)
    outs[0][...] = hidden
    if len(outs) > 1:
        queries = jnp.dot(hidden, query_w_ref[layer + 1], preferred_element_type=jnp.float32)
        queries = (queries / (1.0 + jnp.exp(-queries)) * half_factor).astype(jnp.bfloat16)
        part = queries.shape[1] // (len(outs) - 1)
        for c, out in enumerate(outs[1:]):
            out[...] = queries[:, c * part : (c + 1) * part]


def finish(hidden, gating, gain, w_out, w_query, layer, terms, half_factor, last):
    rows, width = hidden.shape
    flat = [t for group in terms for t in group]
    outs = [jax.ShapeDtypeStruct((rows, width), jnp.bfloat16)]
    if not last:
        outs += [jax.ShapeDtypeStruct((rows, width // CHUNKS), jnp.bfloat16)] * CHUNKS
    return pl.pallas_call(
        functools.partial(finish_kernel, half_factor, layer, [len(group) for group in terms]),
        out_shape=outs,
        cost_estimate=pl.CostEstimate(
            flops=4 * rows * width * width,
            bytes_accessed=4 * width * width,
            transcendentals=rows * width,
        ),
        compiler_params=pltpu.CompilerParams(vmem_limit_bytes=FINISH_VMEM),
    )(hidden, gating, gain, w_out, w_query, *flat)


def per_device(size, targets, hist_keys, hist_values, lengths, cuts, w_query, w_gate, w_out, ln_gain):
    deep = 2 if size % 2 == 0 else 1
    long = size // deep
    paired = long & (long - 1) == 0

    def step_long(z, step):
        return z ^ step if paired else (z + step) % long

    def shift_long(x, step):
        pairs = [(z * deep + y, step_long(z, step) * deep + y) for z in range(long) for y in range(deep)]
        return lax.ppermute(x, "hist", pairs)

    def swap_deep(x):
        pairs = [(z * deep + y, z * deep + (y ^ 1)) for z in range(long) for y in range(deep)]
        return lax.ppermute(x, "hist", pairs)

    hidden = targets[0]
    own_rows, width = hidden.shape
    hist_rows = hist_keys.shape[2]
    layers = hist_keys.shape[0]
    part = width // CHUNKS
    dim = width // HEADS
    half_factor = 0.5 / math.sqrt(dim)
    lims = row_limits(size, deep, step_long, hist_rows, lengths, cuts)

    queries = []
    for c in range(CHUNKS):
        q = jax.nn.silu(
            jnp.dot(
                hidden,
                w_query[0, :, c * part : (c + 1) * part],
                preferred_element_type=jnp.float32,
            )
        )
        queries.append((q * half_factor).astype(jnp.bfloat16))

    for layer in range(layers):
        last = layer == layers - 1
        gating = jax.nn.silu(jnp.dot(hidden, w_gate[layer], preferred_element_type=jnp.float32))
        near, far = [], []
        for c in range(CHUNKS):
            q = queries[c]
            blocks = [q] + [
                shift_long(q, s if paired else -s) for s in range(1, long)
            ]
            near.append(jnp.concatenate(blocks))
            if deep > 1:
                far.append(swap_deep(near[c]))
        terms = []
        before = None
        for c in range(CHUNKS):
            where = (hist_keys, hist_values, layer, c * HEADS // CHUNKS, dim)
            query = near[c]
            if before is not None:
                query, before = lax.optimization_barrier((query, before))
            keep = attend(query, lims[0], *where, jnp.float32)
            before = keep
            if deep > 1:
                query, before = lax.optimization_barrier((far[c], before))
                send = attend(query, lims[1], *where, jnp.bfloat16)
                before = send
                keep = keep + swap_deep(send).astype(jnp.float32)
            group = [keep[:own_rows]]
            for s in range(1, long):
                block = keep[s * own_rows : (s + 1) * own_rows].astype(jnp.bfloat16)
                group.append(shift_long(block, s))
            terms.append(group)
        gain = ln_gain[layer : layer + 1]
        hidden, *queries = finish(
            hidden, gating, gain, w_out, w_query, layer, terms, half_factor, last
        )
    return hidden[None]


def solution(mesh):
    return jax.shard_map(
        functools.partial(per_device, mesh.shape["hist"]),
        mesh=mesh,
        in_specs=(
            P(("groups", "users"), "hist", None),
            P(None, ("groups", "users"), "hist", None),
            P(None, ("groups", "users"), "hist", None),
            P(("groups", "users")),
            P(("groups", "users"), None),
            P(),
            P(),
            P(),
            P(),
        ),
        out_specs=P(("groups", "users"), "hist", None),
        check_vma=False,
    )
```

profile of v0, /device:TPU:0, one launch (start us, length us, event | category | flops | bytes accessed | tf_op | source)
XLA Modules:
  0.0 93.5 jit_solution(356811060429090221)
XLA Ops:
  0.0 1.6 %multiply_convert_fusion.1 = bf16[64,512]{1,0:T(8,128)(2,1)S(1)} fusion(bf16[2,1024,1024]{2,1,0:T(8,128)(2,1)} %query_w_ref.3, bf16[1,64,1024]{2,1,0:T(8,128)(2,1)} %param.9), kind=kOutput, calls=%fused_computation.21 | convolution fusion | flops 67305472 | bytes 1245184 | tf_op jit(solution)/shard_map/dot_general | solution.py:185
  1.6 5.1 %collective-permute-start.2 = (bf16[64,512]{1,0:T(8,128)(2,1)S(1)}, bf16[64,512]{1,0:T(8,128)(2,1)S(1)}, u32[]{:S(2)}, u32[]{:S(2)}) collective-permute-start(bf16[64,512]{1,0:T(8,128)(2,1)S(1)} %multiply_convert_fusion.1), channel_id=1, source_target_pairs={{0,12},{2,14},{4,8},{6,10},{8,4},{10,6},{12,0},{14,2},{1,13},{3,15... | collective-permute-start | bytes 196616 | tf_op jit(solution)/shard_map/ppermute | solution.py:167
  6.8 0.6 collective-permute-start
  7.4 1.6 %multiply_convert_fusion = bf16[64,512]{1,0:T(8,128)(2,1)S(1)} fusion(bf16[2,1024,1024]{2,1,0:T(8,128)(2,1)} %query_w_ref.3, bf16[1,64,1024]{2,1,0:T(8,128)(2,1)} %param.9), kind=kOutput, calls=%fused_computation.20 | convolution fusion | flops 67305472 | bytes 1245184 | tf_op jit(solution)/shard_map/dot_general | solution.py:185
  9.1 3.8 %collective-permute-start.10 = (bf16[64,512]{1,0:T(8,128)(2,1)S(1)}, bf16[64,512]{1,0:T(8,128)(2,1)S(1)}, u32[]{:S(2)}, u32[]{:S(2)}) collective-permute-start(bf16[64,512]{1,0:T(8,128)(2,1)S(1)} %multiply_convert_fusion), channel_id=1, source_target_pairs={{0,12},{2,14},{4,8},{6,10},{8,4},{10,6},{12,0},{14,2},{1,13},{3,15... | collective-permute-start | bytes 196616 | tf_op jit(solution)/shard_map/ppermute | solution.py:167
  13.5 0.7 collective-permute-start.8
  14.3 0.0 slice-start.2
  14.3 0.0 slice-start.1
  14.3 0.0 slice-start.3
  14.3 1.7 %collective-permute-start.3 = (bf16[256,512]{1,0:T(8,128)(2,1)S(1)}, bf16[256,512]{1,0:T(8,128)(2,1)S(1)}, u32[]{:S(2)}, u32[]{:S(2)}) collective-permute-start(bf16[256,512]{1,0:T(8,128)(2,1)S(1)} %pad_maximum_fusion.q_ref), channel_id=1, source_target_pairs={{0,2},{2,0},{4,6},{6,4},{8,10},{10,8},{12,14},{14,12},{1,3},{3,1},... | collective-permute-start | bytes 786440 | tf_op jit(solution)/shard_map/ppermute | solution.py:171
  16.1 0.2 shard_map.91
  16.2 1.9 %collective-permute-done.9 = bf16[64,512]{1,0:T(8,128)(2,1)S(1)} collective-permute-done((bf16[64,512]{1,0:T(8,128)(2,1)S(1)}, bf16[64,512]{1,0:T(8,128)(2,1)S(1)}, u32[]{:S(2)}, u32[]{:S(2)}) %collective-permute-start.9) | collective-permute-done | bytes 65568 | tf_op jit(solution)/shard_map/ppermute | solution.py:167
  18.2 0.6 collective-permute-done.8
  18.8 1.6 %collective-permute-start.11 = (bf16[256,512]{1,0:T(8,128)(2,1)S(1)}, bf16[256,512]{1,0:T(8,128)(2,1)S(1)}, u32[]{:S(2)}, u32[]{:S(2)}) collective-permute-start(bf16[256,512]{1,0:T(8,128)(2,1)S(1)} %pad_maximum_fusion.1.q_ref), channel_id=1, source_target_pairs={{0,2},{2,0},{4,6},{6,4},{8,10},{10,8},{12,14},{14,12},{1,3},{3,1},... | collective-permute-start | bytes 786440 | tf_op jit(solution)/shard_map/ppermute | solution.py:171
  20.4 2.8 %shard_map.92 = f32[256,512]{1,0:T(8,128)S(1)} custom-call(bf16[256,512]{1,0:T(8,128)(2,1)S(1)} %pad_maximum_fusion.q_ref, s32[256,128]{1,0:T(8,128)S(1)} %get-tuple-element.16.lim_ref, bf16[2,1,1536,1024]{3,2,1,0:T(8,128)(2,1)S(1)} %bitcast.30, bf16[2,1,1536,1024]{3,2,1,0:T(8,128)(2,1)S(1)} %bitcast.32), custom_call_target="tpu_custom_call" | custom-call | flops 805306368 | bytes 3670016 | tf_op jit(solution)/shard_map/pallas_call | solution.py:91
  23.2 0.0 copy-start.2
  23.2 2.8 %shard_map.93 = bf16[256,512]{1,0:T(8,128)(2,1)S(1)} custom-call(bf16[256,512]{1,0:T(8,128)(2,1)S(1)} %collective-permute-done.3.q_ref, s32[256,128]{1,0:T(8,128)S(1)} %get-tuple-element.18.lim_ref, bf16[2,1,1536,1024]{3,2,1,0:T(8,128)(2,1)S(1)} %bitcast.30, bf16[2,1,1536,1024]{3,2,1,0:T(8,128)(2,1)S(1)} %bitcast.32), custom_call_target="tpu_custom_call" | custom-call | flops 805306368 | bytes 3670016 | tf_op jit(solution)/shard_map/pallas_call | solution.py:91
  26.0 0.6 collective-permute-start.4
  26.6 0.5 divide_multiply_fusion.1.gate_ref
  27.1 2.8 %shard_map.94 = f32[256,512]{1,0:T(8,128)S(1)} custom-call(bf16[256,512]{1,0:T(8,128)(2,1)S(1)} %pad_maximum_fusion.1.q_ref, s32[256,128]{1,0:T(8,128)S(1)} %get-tuple-element.16.lim_ref, bf16[2,1,1536,1024]{3,2,1,0:T(8,128)(2,1)S(1)} %bitcast.30, bf16[2,1,1536,1024]{3,2,1,0:T(8,128)(2,1)S(1)} %bitcast.32), custom_call_target="tpu_custom_call" | custom-call | flops 805306368 | bytes 3670016 | tf_op jit(solution)/shard_map/pallas_call | solution.py:91
  29.9 2.8 %shard_map.95 = bf16[256,512]{1,0:T(8,128)(2,1)S(1)} custom-call(bf16[256,512]{1,0:T(8,128)(2,1)S(1)} %collective-permute-done.11.q_ref, s32[256,128]{1,0:T(8,128)S(1)} %get-tuple-element.18.lim_ref, bf16[2,1,1536,1024]{3,2,1,0:T(8,128)(2,1)S(1)} %bitcast.30, bf16[2,1,1536,1024]{3,2,1,0:T(8,128)(2,1)S(1)} %bitcast.32), custom_call_target="tpu_custom_call" | custom-call | flops 805306368 | bytes 3670016 | tf_op jit(solution)/shard_map/pallas_call | solution.py:91
  32.7 1.6 %collective-permute-start.12 = (bf16[256,512]{1,0:T(8,128)(2,1)S(1)}, bf16[256,512]{1,0:T(8,128)(2,1)S(1)}, u32[]{:S(2)}, u32[]{:S(2)}) collective-permute-start(bf16[256,512]{1,0:T(8,128)(2,1)S(1)} %shard_map.95), channel_id=1, source_target_pairs={{0,2},{2,0},{4,6},{6,4},{8,10},{10,8},{12,14},{14,12},{1,3},{3,1},... | collective-permute-start | bytes 786440 | tf_op jit(solution)/shard_map/ppermute | solution.py:171
  34.3 0.1 fusion.26
  34.4 1.8 %collective-permute-start.5 = (bf16[64,512]{1,0:T(8,128)(2,1)S(1)}, bf16[64,512]{1,0:T(8,128)(2,1)S(1)}, u32[]{:S(2)}, u32[]{:S(2)}) collective-permute-start(bf16[64,512]{1,0:T(8,128)(2,1)S(1)} %get-tuple-element.46), channel_id=1, source_target_pairs={{0,4},{2,6},{4,0},{6,2},{8,12},{10,14},{12,8},{14,10},{1,5},{3,7},... | collective-permute-start | bytes 196616 | tf_op jit(solution)/shard_map/ppermute | solution.py:167
  36.2 2.2 %collective-permute-start.6 = (bf16[64,512]{1,0:T(8,128)(2,1)S(1)}, bf16[64,512]{1,0:T(8,128)(2,1)S(1)}, u32[]{:S(2)}, u32[]{:S(2)}) collective-permute-start(bf16[64,512]{1,0:T(8,128)(2,1)S(1)} %get-tuple-element.45), channel_id=1, source_target_pairs={{0,8},{2,10},{4,12},{6,14},{8,0},{10,2},{12,4},{14,6},{1,9},{3,11}... | collective-permute-start | bytes 196616 | tf_op jit(solution)/shard_map/ppermute | solution.py:167
  38.4 0.5 collective-permute-start.7
  38.9 0.3 collective-permute-done.12
  39.1 0.1 fusion.25
  39.3 2.8 %collective-permute-start.13 = (bf16[64,512]{1,0:T(8,128)(2,1)S(1)}, bf16[64,512]{1,0:T(8,128)(2,1)S(1)}, u32[]{:S(2)}, u32[]{:S(2)}) collective-permute-start(bf16[64,512]{1,0:T(8,128)(2,1)S(1)} %get-tuple-element.43), channel_id=1, source_target_pairs={{0,4},{2,6},{4,0},{6,2},{8,12},{10,14},{12,8},{14,10},{1,5},{3,7},... | collective-permute-start | bytes 196616 | tf_op jit(solution)/shard_map/ppermute | solution.py:167
  42.0 2.2 %collective-permute-start.14 = (bf16[64,512]{1,0:T(8,128)(2,1)S(1)}, bf16[64,512]{1,0:T(8,128)(2,1)S(1)}, u32[]{:S(2)}, u32[]{:S(2)}) collective-permute-start(bf16[64,512]{1,0:T(8,128)(2,1)S(1)} %get-tuple-element.42), channel_id=1, source_target_pairs={{0,8},{2,10},{4,12},{6,14},{8,0},{10,2},{12,4},{14,6},{1,9},{3,11}... | collective-permute-start | bytes 196616 | tf_op jit(solution)/shard_map/ppermute | solution.py:167
  44.2 0.3 collective-permute-start.15
  44.5 0.7 collective-permute-done.7.refs_3_
  45.2 0.5 collective-permute-done.13.refs_5_
  45.7 2.2 %collective-permute-done.14.refs_6_ = bf16[64,512]{1,0:T(8,128)(2,1)S(1)} collective-permute-done((bf16[64,512]{1,0:T(8,128)(2,1)S(1)}, bf16[64,512]{1,0:T(8,128)(2,1)S(1)}, u32[]{:S(2)}, u32[]{:S(2)}) %collective-permute-start.14) | collective-permute-done | bytes 65568 | tf_op jit(solution)/shard_map/ppermute | solution.py:167
  47.9 2.5 %collective-permute-done.15.refs_7_ = bf16[64,512]{1,0:T(8,128)(2,1)S(1)} collective-permute-done((bf16[64,512]{1,0:T(8,128)(2,1)S(1)}, bf16[64,512]{1,0:T(8,128)(2,1)S(1)}, u32[]{:S(2)}, u32[]{:S(2)}) %collective-permute-start.15) | collective-permute-done | bytes 65568 | tf_op jit(solution)/shard_map/ppermute | solution.py:167
  50.4 1.1 %shard_map.96 = (bf16[64,1024]{1,0:T(8,128)(2,1)S(1)}, bf16[64,512]{1,0:T(8,128)(2,1)S(1)}, bf16[64,512]{1,0:T(8,128)(2,1)S(1)}) custom-call(bf16[64,1024]{1,0:T(8,128)(2,1)S(1)} %bitcast.33, f32[64,1024]{1,0:T(8,128)S(1)} %divide_multiply_fusion.1.gate_ref, f32[1,1024]{1,0:T(1,128)S(1)} %get-tuple-element.48.gain_ref, bf16[2,1024,1024]{2,1,0:T(8,128)(2,1)S(1)} %copy-done, ...), custom_call_target="tpu_custom_call" | custom-call | flops 268435456 | bytes 4194304 | tf_op jit(solution)/shard_map/pallas_call | solution.py:145
  51.5 0.1 collective-permute-start.16
  51.6 1.3 %collective-permute-start.17 = (bf16[64,512]{1,0:T(8,128)(2,1)S(1)}, bf16[64,512]{1,0:T(8,128)(2,1)S(1)}, u32[]{:S(2)}, u32[]{:S(2)}) collective-permute-start(bf16[64,512]{1,0:T(8,128)(2,1)S(1)} %get-tuple-element.22), channel_id=1, source_target_pairs={{0,8},{2,10},{4,12},{6,14},{8,0},{10,2},{12,4},{14,6},{1,9},{3,11}... | collective-permute-start | bytes 196616 | tf_op jit(solution)/shard_map/ppermute | solution.py:167
  52.8 3.1 %collective-permute-start.18 = (bf16[64,512]{1,0:T(8,128)(2,1)S(1)}, bf16[64,512]{1,0:T(8,128)(2,1)S(1)}, u32[]{:S(2)}, u32[]{:S(2)}) collective-permute-start(bf16[64,512]{1,0:T(8,128)(2,1)S(1)} %get-tuple-element.22), channel_id=1, source_target_pairs={{0,12},{2,14},{4,8},{6,10},{8,4},{10,6},{12,0},{14,2},{1,13},{3,15... | collective-permute-start | bytes 196616 | tf_op jit(solution)/shard_map/ppermute | solution.py:167
  55.9 1.3 %collective-permute-start.25 = (bf16[64,512]{1,0:T(8,128)(2,1)S(1)}, bf16[64,512]{1,0:T(8,128)(2,1)S(1)}, u32[]{:S(2)}, u32[]{:S(2)}) collective-permute-start(bf16[64,512]{1,0:T(8,128)(2,1)S(1)} %get-tuple-element.24), channel_id=1, source_target_pairs={{0,8},{2,10},{4,12},{6,14},{8,0},{10,2},{12,4},{14,6},{1,9},{3,11}... | collective-permute-start | bytes 196616 | tf_op jit(solution)/shard_map/ppermute | solution.py:167
  57.2 3.2 %collective-permute-start.26 = (bf16[64,512]{1,0:T(8,128)(2,1)S(1)}, bf16[64,512]{1,0:T(8,128)(2,1)S(1)}, u32[]{:S(2)}, u32[]{:S(2)}) collective-permute-start(bf16[64,512]{1,0:T(8,128)(2,1)S(1)} %get-tuple-element.24), channel_id=1, source_target_pairs={{0,12},{2,14},{4,8},{6,10},{8,4},{10,6},{12,0},{14,2},{1,13},{3,15... | collective-permute-start | bytes 196616 | tf_op jit(solution)/shard_map/ppermute | solution.py:167
  60.4 0.6 collective-permute-start.19
  61.1 0.0 collective-permute-done.25
  61.1 2.7 %shard_map.97 = f32[256,512]{1,0:T(8,128)S(1)} custom-call(bf16[256,512]{1,0:T(8,128)(2,1)S(1)} %constant_dynamic-update-slice_fusion.q_ref, s32[256,128]{1,0:T(8,128)S(1)} %get-tuple-element.16.lim_ref, bf16[2,1,1536,1024]{3,2,1,0:T(8,128)(2,1)S(1)} %bitcast.30, bf16[2,1,1536,1024]{3,2,1,0:T(8,128)(2,1)S(1)} %bitcast.32), custom_call_target="tpu_custom_call" | custom-call | flops 805306368 | bytes 3670016 | tf_op jit(solution)/shard_map/pallas_call | solution.py:91
  63.9 1.6 %collective-permute-start.27 = (bf16[256,512]{1,0:T(8,128)(2,1)S(1)}, bf16[256,512]{1,0:T(8,128)(2,1)S(1)}, u32[]{:S(2)}, u32[]{:S(2)}) collective-permute-start(bf16[256,512]{1,0:T(8,128)(2,1)S(1)} %constant_dynamic-update-slice_fusion.4.q_ref), channel_id=1, source_target_pairs={{0,2},{2,0},{4,6},{6,4},{8,10},{10,8},{12,14},{14,12},{1,3},{3,1},... | collective-permute-start | bytes 786440 | tf_op jit(solution)/shard_map/ppermute | solution.py:171
  65.4 3.9 %collective-permute-done.19.q_ref = bf16[256,512]{1,0:T(8,128)(2,1)S(1)} collective-permute-done((bf16[256,512]{1,0:T(8,128)(2,1)S(1)}, bf16[256,512]{1,0:T(8,128)(2,1)S(1)}, u32[]{:S(2)}, u32[]{:S(2)}) %collective-permute-start.19) | collective-permute-done | bytes 262176 | tf_op jit(solution)/shard_map/ppermute | solution.py:171
  69.3 2.7 %shard_map.98 = bf16[256,512]{1,0:T(8,128)(2,1)S(1)} custom-call(bf16[256,512]{1,0:T(8,128)(2,1)S(1)} %collective-permute-done.19.q_ref, s32[256,128]{1,0:T(8,128)S(1)} %get-tuple-element.18.lim_ref, bf16[2,1,1536,1024]{3,2,1,0:T(8,128)(2,1)S(1)} %bitcast.30, bf16[2,1,1536,1024]{3,2,1,0:T(8,128)(2,1)S(1)} %bitcast.32), custom_call_target="tpu_custom_call" | custom-call | flops 805306368 | bytes 3670016 | tf_op jit(solution)/shard_map/pallas_call | solution.py:91
  72.1 0.4 collective-permute-start.20
  72.5 2.8 %shard_map.99 = f32[256,512]{1,0:T(8,128)S(1)} custom-call(bf16[256,512]{1,0:T(8,128)(2,1)S(1)} %constant_dynamic-update-slice_fusion.4.q_ref, s32[256,128]{1,0:T(8,128)S(1)} %get-tuple-element.16.lim_ref, bf16[2,1,1536,1024]{3,2,1,0:T(8,128)(2,1)S(1)} %bitcast.30, bf16[2,1,1536,1024]{3,2,1,0:T(8,128)(2,1)S(1)} %bitcast.32), custom_call_target="tpu_custom_call" | custom-call | flops 805306368 | bytes 3670016 | tf_op jit(solution)/shard_map/pallas_call | solution.py:91
  75.2 2.8 %shard_map.100 = bf16[256,512]{1,0:T(8,128)(2,1)S(1)} custom-call(bf16[256,512]{1,0:T(8,128)(2,1)S(1)} %collective-permute-done.27.q_ref, s32[256,128]{1,0:T(8,128)S(1)} %get-tuple-element.18.lim_ref, bf16[2,1,1536,1024]{3,2,1,0:T(8,128)(2,1)S(1)} %bitcast.30, bf16[2,1,1536,1024]{3,2,1,0:T(8,128)(2,1)S(1)} %bitcast.32), custom_call_target="tpu_custom_call" | custom-call | flops 805306368 | bytes 3670016 | tf_op jit(solution)/shard_map/pallas_call | solution.py:91
  78.0 1.8 %collective-permute-start.28 = (bf16[256,512]{1,0:T(8,128)(2,1)S(1)}, bf16[256,512]{1,0:T(8,128)(2,1)S(1)}, u32[]{:S(2)}, u32[]{:S(2)}) collective-permute-start(bf16[256,512]{1,0:T(8,128)(2,1)S(1)} %shard_map.100), channel_id=1, source_target_pairs={{0,2},{2,0},{4,6},{6,4},{8,10},{10,8},{12,14},{14,12},{1,3},{3,1},... | collective-permute-start | bytes 786440 | tf_op jit(solution)/shard_map/ppermute | solution.py:171
  79.8 0.1 fusion.24
  79.9 0.1 collective-permute-start.21
  80.0 1.2 %collective-permute-start.22 = (bf16[64,512]{1,0:T(8,128)(2,1)S(1)}, bf16[64,512]{1,0:T(8,128)(2,1)S(1)}, u32[]{:S(2)}, u32[]{:S(2)}) collective-permute-start(bf16[64,512]{1,0:T(8,128)(2,1)S(1)} %get-tuple-element.39), channel_id=1, source_target_pairs={{0,8},{2,10},{4,12},{6,14},{8,0},{10,2},{12,4},{14,6},{1,9},{3,11}... | collective-permute-start | bytes 196616 | tf_op jit(solution)/shard_map/ppermute | solution.py:167
  81.2 3.2 %collective-permute-start.23 = (bf16[64,512]{1,0:T(8,128)(2,1)S(1)}, bf16[64,512]{1,0:T(8,128)(2,1)S(1)}, u32[]{:S(2)}, u32[]{:S(2)}) collective-permute-start(bf16[64,512]{1,0:T(8,128)(2,1)S(1)} %get-tuple-element.38), channel_id=1, source_target_pairs={{0,12},{2,14},{4,8},{6,10},{8,4},{10,6},{12,0},{14,2},{1,13},{3,15... | collective-permute-start | bytes 196616 | tf_op jit(solution)/shard_map/ppermute | solution.py:167
  84.3 0.1 collective-permute-done.28
  84.5 0.1 fusion.23
  84.6 0.1 collective-permute-start.29
  84.6 1.5 %collective-permute-start.30 = (bf16[64,512]{1,0:T(8,128)(2,1)S(1)}, bf16[64,512]{1,0:T(8,128)(2,1)S(1)}, u32[]{:S(2)}, u32[]{:S(2)}) collective-permute-start(bf16[64,512]{1,0:T(8,128)(2,1)S(1)} %get-tuple-element.36), channel_id=1, source_target_pairs={{0,8},{2,10},{4,12},{6,14},{8,0},{10,2},{12,4},{14,6},{1,9},{3,11}... | collective-permute-start | bytes 196616 | tf_op jit(solution)/shard_map/ppermute | solution.py:167
  86.2 2.9 %collective-permute-start.31 = (bf16[64,512]{1,0:T(8,128)(2,1)S(1)}, bf16[64,512]{1,0:T(8,128)(2,1)S(1)}, u32[]{:S(2)}, u32[]{:S(2)}) collective-permute-start(bf16[64,512]{1,0:T(8,128)(2,1)S(1)} %get-tuple-element.35), channel_id=1, source_target_pairs={{0,12},{2,14},{4,8},{6,10},{8,4},{10,6},{12,0},{14,2},{1,13},{3,15... | collective-permute-start | bytes 196616 | tf_op jit(solution)/shard_map/ppermute | solution.py:167
  89.0 0.5 divide_multiply_fusion.gate_ref
  89.6 0.3 collective-permute-done.30.refs_6_
  89.9 2.3 %collective-permute-done.31.refs_7_ = bf16[64,512]{1,0:T(8,128)(2,1)S(1)} collective-permute-done((bf16[64,512]{1,0:T(8,128)(2,1)S(1)}, bf16[64,512]{1,0:T(8,128)(2,1)S(1)}, u32[]{:S(2)}, u32[]{:S(2)}) %collective-permute-start.31) | collective-permute-done | bytes 65568 | tf_op jit(solution)/shard_map/ppermute | solution.py:167
  92.2 1.3 %shard_map.101 = bf16[64,1024]{1,0:T(8,128)(2,1)} custom-call(bf16[64,1024]{1,0:T(8,128)(2,1)S(1)} %get-tuple-element.21.hidden_ref, f32[64,1024]{1,0:T(8,128)S(1)} %divide_multiply_fusion.gate_ref, f32[1,1024]{1,0:T(1,128)S(1)} %get-tuple-element.47.gain_ref, bf16[2,1024,1024]{2,1,0:T(8,128)(2,1)S(1)} %copy-done, bf16[2,1024,1024]{2,1,0:T(8,128)(2,1)S(1)} %copy-done.1, ...), custom_call_target="tpu_custom_call" | custom-call | flops 268435456 | bytes 4194304 | tf_op jit(solution)/shard_map/pallas_call | solution.py:145
  (60 shorter events, 0.3 us)
Async XLA Ops:
  0.0 16.1 %copy-start.3 = (s32[1,512]{1,0:T(1,128)S(1)}, s32[1,512]{1,0:T(1,128)}, u32[]{:S(2)}) copy-start(s32[1,512]{1,0:T(1,128)} %cuts_ref.1) | copy-start | bytes 6148
  1.6 11.9 %collective-permute-start.2 = (bf16[64,512]{1,0:T(8,128)(2,1)S(1)}, bf16[64,512]{1,0:T(8,128)(2,1)S(1)}, u32[]{:S(2)}, u32[]{:S(2)}) collective-permute-start(bf16[64,512]{1,0:T(8,128)(2,1)S(1)} %multiply_convert_fusion.1), channel_id=1, source_target_pairs={{0,12},{2,14},{4,8},{6,10},{8,4},{10,6},{12,0},{14,2},{1,13},{3,15... | collective-permute-start | bytes 196616 | tf_op jit(solution)/shard_map/ppermute | solution.py:167
  6.8 7.5 %collective-permute-start.1 = (bf16[64,512]{1,0:T(8,128)(2,1)S(1)}, bf16[64,512]{1,0:T(8,128)(2,1)S(1)}, u32[]{:S(2)}, u32[]{:S(2)}) collective-permute-start(bf16[64,512]{1,0:T(8,128)(2,1)S(1)} %multiply_convert_fusion.1), channel_id=1, source_target_pairs={{0,8},{2,10},{4,12},{6,14},{8,0},{10,2},{12,4},{14,6},{1,9},{3,11}... | collective-permute-start | bytes 196616 | tf_op jit(solution)/shard_map/ppermute | solution.py:167
  6.8 7.5 %collective-permute-start = (bf16[64,512]{1,0:T(8,128)(2,1)S(1)}, bf16[64,512]{1,0:T(8,128)(2,1)S(1)}, u32[]{:S(2)}, u32[]{:S(2)}) collective-permute-start(bf16[64,512]{1,0:T(8,128)(2,1)S(1)} %multiply_convert_fusion.1), channel_id=1, source_target_pairs={{0,4},{2,6},{4,0},{6,2},{8,12},{10,14},{12,8},{14,10},{1,5},{3,7},... | collective-permute-start | bytes 196616 | tf_op jit(solution)/shard_map/ppermute | solution.py:167
  9.1 7.2 %collective-permute-start.10 = (bf16[64,512]{1,0:T(8,128)(2,1)S(1)}, bf16[64,512]{1,0:T(8,128)(2,1)S(1)}, u32[]{:S(2)}, u32[]{:S(2)}) collective-permute-start(bf16[64,512]{1,0:T(8,128)(2,1)S(1)} %multiply_convert_fusion), channel_id=1, source_target_pairs={{0,12},{2,14},{4,8},{6,10},{8,4},{10,6},{12,0},{14,2},{1,13},{3,15... | collective-permute-start | bytes 196616 | tf_op jit(solution)/shard_map/ppermute | solution.py:167
  12.9 5.3 %collective-permute-start.9 = (bf16[64,512]{1,0:T(8,128)(2,1)S(1)}, bf16[64,512]{1,0:T(8,128)(2,1)S(1)}, u32[]{:S(2)}, u32[]{:S(2)}) collective-permute-start(bf16[64,512]{1,0:T(8,128)(2,1)S(1)} %multiply_convert_fusion), channel_id=1, source_target_pairs={{0,8},{2,10},{4,12},{6,14},{8,0},{10,2},{12,4},{14,6},{1,9},{3,11}... | collective-permute-start | bytes 196616 | tf_op jit(solution)/shard_map/ppermute | solution.py:167
  13.5 5.2 %collective-permute-start.8 = (bf16[64,512]{1,0:T(8,128)(2,1)S(1)}, bf16[64,512]{1,0:T(8,128)(2,1)S(1)}, u32[]{:S(2)}, u32[]{:S(2)}) collective-permute-start(bf16[64,512]{1,0:T(8,128)(2,1)S(1)} %multiply_convert_fusion), channel_id=1, source_target_pairs={{0,4},{2,6},{4,0},{6,2},{8,12},{10,14},{12,8},{14,10},{1,5},{3,7},... | collective-permute-start | bytes 196616 | tf_op jit(solution)/shard_map/ppermute | solution.py:167
  14.3 6.1 %slice-start = ((s8[6291456]{0:T(1024)(128)(4,1)}), s8[4194304]{0:T(1024)(128)(4,1)S(1)}, s32[]{:S(2)}) async-start(s8[6291456]{0:T(1024)(128)(4,1)} %bitcast.29), calls=%async_computation | async-start | bytes 8388608
  14.3 6.1 %slice-start.2 = ((s8[6291456]{0:T(1024)(128)(4,1)}), s8[4194304]{0:T(1024)(128)(4,1)S(1)}, s32[]{:S(2)}) async-start(s8[6291456]{0:T(1024)(128)(4,1)} %bitcast.31), calls=%async_computation.2 | async-start | bytes 8388608
  14.3 6.1 %slice-start.1 = ((s8[6291456]{0:T(1024)(128)(4,1)}), s8[2097152]{0:T(1024)(128)(4,1)S(1)}, s32[]{:S(2)}) async-start(s8[6291456]{0:T(1024)(128)(4,1)} %bitcast.29), calls=%async_computation.1 | async-start | bytes 4194304
  14.3 6.1 %slice-start.3 = ((s8[6291456]{0:T(1024)(128)(4,1)}), s8[2097152]{0:T(1024)(128)(4,1)S(1)}, s32[]{:S(2)}) async-start(s8[6291456]{0:T(1024)(128)(4,1)} %bitcast.31), calls=%async_computation.3 | async-start | bytes 4194304
  14.3 8.9 %collective-permute-start.3 = (bf16[256,512]{1,0:T(8,128)(2,1)S(1)}, bf16[256,512]{1,0:T(8,128)(2,1)S(1)}, u32[]{:S(2)}, u32[]{:S(2)}) collective-permute-start(bf16[256,512]{1,0:T(8,128)(2,1)S(1)} %pad_maximum_fusion.q_ref), channel_id=1, source_target_pairs={{0,2},{2,0},{4,6},{6,4},{8,10},{10,8},{12,14},{14,12},{1,3},{3,1},... | collective-permute-start | bytes 786440 | tf_op jit(solution)/shard_map/ppermute | solution.py:171
  18.8 11.1 %collective-permute-start.11 = (bf16[256,512]{1,0:T(8,128)(2,1)S(1)}, bf16[256,512]{1,0:T(8,128)(2,1)S(1)}, u32[]{:S(2)}, u32[]{:S(2)}) collective-permute-start(bf16[256,512]{1,0:T(8,128)(2,1)S(1)} %pad_maximum_fusion.1.q_ref), channel_id=1, source_target_pairs={{0,2},{2,0},{4,6},{6,4},{8,10},{10,8},{12,14},{14,12},{1,3},{3,1},... | collective-permute-start | bytes 786440 | tf_op jit(solution)/shard_map/ppermute | solution.py:171
  23.2 3.4 %copy-start.2 = (bf16[1,64,1024]{2,1,0:T(8,128)(2,1)S(1)}, bf16[1,64,1024]{2,1,0:T(8,128)(2,1)}, u32[]{:S(2)}) copy-start(bf16[1,64,1024]{2,1,0:T(8,128)(2,1)} %param.9) | copy-start | bytes 393220
  23.2 3.4 %copy-start.5 = (bf16[2,1024,1024]{2,1,0:T(8,128)(2,1)S(1)}, bf16[2,1024,1024]{2,1,0:T(8,128)(2,1)}, u32[]{:S(2)}) copy-start(bf16[2,1024,1024]{2,1,0:T(8,128)(2,1)} %param.15) | copy-start | bytes 12582916
  26.0 8.3 %collective-permute-start.4 = (bf16[256,512]{1,0:T(8,128)(2,1)S(1)}, bf16[256,512]{1,0:T(8,128)(2,1)S(1)}, u32[]{:S(2)}, u32[]{:S(2)}) collective-permute-start(bf16[256,512]{1,0:T(8,128)(2,1)S(1)} %shard_map.93), channel_id=1, source_target_pairs={{0,2},{2,0},{4,6},{6,4},{8,10},{10,8},{12,14},{14,12},{1,3},{3,1},... | collective-permute-start | bytes 786440 | tf_op jit(solution)/shard_map/ppermute | solution.py:171
  29.9 14.6 %copy-start.4 = (f32[2,1024]{1,0:T(2,128)S(1)}, f32[2,1024]{1,0:T(2,128)}, u32[]{:S(2)}) copy-start(f32[2,1024]{1,0:T(2,128)} %param.17) | copy-start | bytes 24580
  29.9 20.5 %copy-start.1 = (bf16[2,1024,1024]{2,1,0:T(8,128)(2,1)S(1)}, bf16[2,1024,1024]{2,1,0:T(8,128)(2,1)}, u32[]{:S(2)}) copy-start(bf16[2,1024,1024]{2,1,0:T(8,128)(2,1)} %query_w_ref.3) | copy-start | bytes 12582916
  32.7 17.7 %copy-start = (bf16[2,1024,1024]{2,1,0:T(8,128)(2,1)S(1)}, bf16[2,1024,1024]{2,1,0:T(8,128)(2,1)}, u32[]{:S(2)}) copy-start(bf16[2,1024,1024]{2,1,0:T(8,128)(2,1)} %out_w_ref.3) | copy-start | bytes 12582916
  32.7 6.5 %collective-permute-start.12 = (bf16[256,512]{1,0:T(8,128)(2,1)S(1)}, bf16[256,512]{1,0:T(8,128)(2,1)S(1)}, u32[]{:S(2)}, u32[]{:S(2)}) collective-permute-start(bf16[256,512]{1,0:T(8,128)(2,1)S(1)} %shard_map.95), channel_id=1, source_target_pairs={{0,2},{2,0},{4,6},{6,4},{8,10},{10,8},{12,14},{14,12},{1,3},{3,1},... | collective-permute-start | bytes 786440 | tf_op jit(solution)/shard_map/ppermute | solution.py:171
  34.4 9.8 %collective-permute-start.5 = (bf16[64,512]{1,0:T(8,128)(2,1)S(1)}, bf16[64,512]{1,0:T(8,128)(2,1)S(1)}, u32[]{:S(2)}, u32[]{:S(2)}) collective-permute-start(bf16[64,512]{1,0:T(8,128)(2,1)S(1)} %get-tuple-element.46), channel_id=1, source_target_pairs={{0,4},{2,6},{4,0},{6,2},{8,12},{10,14},{12,8},{14,10},{1,5},{3,7},... | collective-permute-start | bytes 196616 | tf_op jit(solution)/shard_map/ppermute | solution.py:167
  36.2 8.3 %collective-permute-start.6 = (bf16[64,512]{1,0:T(8,128)(2,1)S(1)}, bf16[64,512]{1,0:T(8,128)(2,1)S(1)}, u32[]{:S(2)}, u32[]{:S(2)}) collective-permute-start(bf16[64,512]{1,0:T(8,128)(2,1)S(1)} %get-tuple-element.45), channel_id=1, source_target_pairs={{0,8},{2,10},{4,12},{6,14},{8,0},{10,2},{12,4},{14,6},{1,9},{3,11}... | collective-permute-start | bytes 196616 | tf_op jit(solution)/shard_map/ppermute | solution.py:167
  38.4 6.8 %collective-permute-start.7 = (bf16[64,512]{1,0:T(8,128)(2,1)S(1)}, bf16[64,512]{1,0:T(8,128)(2,1)S(1)}, u32[]{:S(2)}, u32[]{:S(2)}) collective-permute-start(bf16[64,512]{1,0:T(8,128)(2,1)S(1)} %get-tuple-element.44), channel_id=1, source_target_pairs={{0,12},{2,14},{4,8},{6,10},{8,4},{10,6},{12,0},{14,2},{1,13},{3,15... | collective-permute-start | bytes 196616 | tf_op jit(solution)/shard_map/ppermute | solution.py:167
  39.3 6.4 %collective-permute-start.13 = (bf16[64,512]{1,0:T(8,128)(2,1)S(1)}, bf16[64,512]{1,0:T(8,128)(2,1)S(1)}, u32[]{:S(2)}, u32[]{:S(2)}) collective-permute-start(bf16[64,512]{1,0:T(8,128)(2,1)S(1)} %get-tuple-element.43), channel_id=1, source_target_pairs={{0,4},{2,6},{4,0},{6,2},{8,12},{10,14},{12,8},{14,10},{1,5},{3,7},... | collective-permute-start | bytes 196616 | tf_op jit(solution)/shard_map/ppermute | solution.py:167
  42.0 5.8 %collective-permute-start.14 = (bf16[64,512]{1,0:T(8,128)(2,1)S(1)}, bf16[64,512]{1,0:T(8,128)(2,1)S(1)}, u32[]{:S(2)}, u32[]{:S(2)}) collective-permute-start(bf16[64,512]{1,0:T(8,128)(2,1)S(1)} %get-tuple-element.42), channel_id=1, source_target_pairs={{0,8},{2,10},{4,12},{6,14},{8,0},{10,2},{12,4},{14,6},{1,9},{3,11}... | collective-permute-start | bytes 196616 | tf_op jit(solution)/shard_map/ppermute | solution.py:167
  44.2 6.2 %collective-permute-start.15 = (bf16[64,512]{1,0:T(8,128)(2,1)S(1)}, bf16[64,512]{1,0:T(8,128)(2,1)S(1)}, u32[]{:S(2)}, u32[]{:S(2)}) collective-permute-start(bf16[64,512]{1,0:T(8,128)(2,1)S(1)} %get-tuple-element.41), channel_id=1, source_target_pairs={{0,12},{2,14},{4,8},{6,10},{8,4},{10,6},{12,0},{14,2},{1,13},{3,15... | collective-permute-start | bytes 196616 | tf_op jit(solution)/shard_map/ppermute | solution.py:167
  51.5 5.7 %collective-permute-start.16 = (bf16[64,512]{1,0:T(8,128)(2,1)S(1)}, bf16[64,512]{1,0:T(8,128)(2,1)S(1)}, u32[]{:S(2)}, u32[]{:S(2)}) collective-permute-start(bf16[64,512]{1,0:T(8,128)(2,1)S(1)} %get-tuple-element.22), channel_id=1, source_target_pairs={{0,4},{2,6},{4,0},{6,2},{8,12},{10,14},{12,8},{14,10},{1,5},{3,7},... | collective-permute-start | bytes 196616 | tf_op jit(solution)/shard_map/ppermute | solution.py:167
  51.6 8.8 %collective-permute-start.17 = (bf16[64,512]{1,0:T(8,128)(2,1)S(1)}, bf16[64,512]{1,0:T(8,128)(2,1)S(1)}, u32[]{:S(2)}, u32[]{:S(2)}) collective-permute-start(bf16[64,512]{1,0:T(8,128)(2,1)S(1)} %get-tuple-element.22), channel_id=1, source_target_pairs={{0,8},{2,10},{4,12},{6,14},{8,0},{10,2},{12,4},{14,6},{1,9},{3,11}... | collective-permute-start | bytes 196616 | tf_op jit(solution)/shard_map/ppermute | solution.py:167
  52.8 7.6 %collective-permute-start.18 = (bf16[64,512]{1,0:T(8,128)(2,1)S(1)}, bf16[64,512]{1,0:T(8,128)(2,1)S(1)}, u32[]{:S(2)}, u32[]{:S(2)}) collective-permute-start(bf16[64,512]{1,0:T(8,128)(2,1)S(1)} %get-tuple-element.22), channel_id=1, source_target_pairs={{0,12},{2,14},{4,8},{6,10},{8,4},{10,6},{12,0},{14,2},{1,13},{3,15... | collective-permute-start | bytes 196616 | tf_op jit(solution)/shard_map/ppermute | solution.py:167
  55.9 5.1 %collective-permute-start.24 = (bf16[64,512]{1,0:T(8,128)(2,1)S(1)}, bf16[64,512]{1,0:T(8,128)(2,1)S(1)}, u32[]{:S(2)}, u32[]{:S(2)}) collective-permute-start(bf16[64,512]{1,0:T(8,128)(2,1)S(1)} %get-tuple-element.24), channel_id=1, source_target_pairs={{0,4},{2,6},{4,0},{6,2},{8,12},{10,14},{12,8},{14,10},{1,5},{3,7},... | collective-permute-start | bytes 196616 | tf_op jit(solution)/shard_map/ppermute | solution.py:167
  55.9 5.2 %collective-permute-start.25 = (bf16[64,512]{1,0:T(8,128)(2,1)S(1)}, bf16[64,512]{1,0:T(8,128)(2,1)S(1)}, u32[]{:S(2)}, u32[]{:S(2)}) collective-permute-start(bf16[64,512]{1,0:T(8,128)(2,1)S(1)} %get-tuple-element.24), channel_id=1, source_target_pairs={{0,8},{2,10},{4,12},{6,14},{8,0},{10,2},{12,4},{14,6},{1,9},{3,11}... | collective-permute-start | bytes 196616 | tf_op jit(solution)/shard_map/ppermute | solution.py:167
  57.2 6.6 %collective-permute-start.26 = (bf16[64,512]{1,0:T(8,128)(2,1)S(1)}, bf16[64,512]{1,0:T(8,128)(2,1)S(1)}, u32[]{:S(2)}, u32[]{:S(2)}) collective-permute-start(bf16[64,512]{1,0:T(8,128)(2,1)S(1)} %get-tuple-element.24), channel_id=1, source_target_pairs={{0,12},{2,14},{4,8},{6,10},{8,4},{10,6},{12,0},{14,2},{1,13},{3,15... | collective-permute-start | bytes 196616 | tf_op jit(solution)/shard_map/ppermute | solution.py:167
  60.4 8.9 %collective-permute-start.19 = (bf16[256,512]{1,0:T(8,128)(2,1)S(1)}, bf16[256,512]{1,0:T(8,128)(2,1)S(1)}, u32[]{:S(2)}, u32[]{:S(2)}) collective-permute-start(bf16[256,512]{1,0:T(8,128)(2,1)S(1)} %constant_dynamic-update-slice_fusion.q_ref), channel_id=1, source_target_pairs={{0,2},{2,0},{4,6},{6,4},{8,10},{10,8},{12,14},{14,12},{1,3},{3,1},... | collective-permute-start | bytes 786440 | tf_op jit(solution)/shard_map/ppermute | solution.py:171
  63.9 11.4 %collective-permute-start.27 = (bf16[256,512]{1,0:T(8,128)(2,1)S(1)}, bf16[256,512]{1,0:T(8,128)(2,1)S(1)}, u32[]{:S(2)}, u32[]{:S(2)}) collective-permute-start(bf16[256,512]{1,0:T(8,128)(2,1)S(1)} %constant_dynamic-update-slice_fusion.4.q_ref), channel_id=1, source_target_pairs={{0,2},{2,0},{4,6},{6,4},{8,10},{10,8},{12,14},{14,12},{1,3},{3,1},... | collective-permute-start | bytes 786440 | tf_op jit(solution)/shard_map/ppermute | solution.py:171
  72.1 7.7 %collective-permute-start.20 = (bf16[256,512]{1,0:T(8,128)(2,1)S(1)}, bf16[256,512]{1,0:T(8,128)(2,1)S(1)}, u32[]{:S(2)}, u32[]{:S(2)}) collective-permute-start(bf16[256,512]{1,0:T(8,128)(2,1)S(1)} %shard_map.98), channel_id=1, source_target_pairs={{0,2},{2,0},{4,6},{6,4},{8,10},{10,8},{12,14},{14,12},{1,3},{3,1},... | collective-permute-start | bytes 786440 | tf_op jit(solution)/shard_map/ppermute | solution.py:171
  78.0 6.4 %collective-permute-start.28 = (bf16[256,512]{1,0:T(8,128)(2,1)S(1)}, bf16[256,512]{1,0:T(8,128)(2,1)S(1)}, u32[]{:S(2)}, u32[]{:S(2)}) collective-permute-start(bf16[256,512]{1,0:T(8,128)(2,1)S(1)} %shard_map.100), channel_id=1, source_target_pairs={{0,2},{2,0},{4,6},{6,4},{8,10},{10,8},{12,14},{14,12},{1,3},{3,1},... | collective-permute-start | bytes 786440 | tf_op jit(solution)/shard_map/ppermute | solution.py:171
  79.9 6.3 %collective-permute-start.21 = (bf16[64,512]{1,0:T(8,128)(2,1)S(1)}, bf16[64,512]{1,0:T(8,128)(2,1)S(1)}, u32[]{:S(2)}, u32[]{:S(2)}) collective-permute-start(bf16[64,512]{1,0:T(8,128)(2,1)S(1)} %get-tuple-element.40), channel_id=1, source_target_pairs={{0,4},{2,6},{4,0},{6,2},{8,12},{10,14},{12,8},{14,10},{1,5},{3,7},... | collective-permute-start | bytes 196616 | tf_op jit(solution)/shard_map/ppermute | solution.py:167
  80.0 9.6 %collective-permute-start.22 = (bf16[64,512]{1,0:T(8,128)(2,1)S(1)}, bf16[64,512]{1,0:T(8,128)(2,1)S(1)}, u32[]{:S(2)}, u32[]{:S(2)}) collective-permute-start(bf16[64,512]{1,0:T(8,128)(2,1)S(1)} %get-tuple-element.39), channel_id=1, source_target_pairs={{0,8},{2,10},{4,12},{6,14},{8,0},{10,2},{12,4},{14,6},{1,9},{3,11}... | collective-permute-start | bytes 196616 | tf_op jit(solution)/shard_map/ppermute | solution.py:167
  81.2 8.4 %collective-permute-start.23 = (bf16[64,512]{1,0:T(8,128)(2,1)S(1)}, bf16[64,512]{1,0:T(8,128)(2,1)S(1)}, u32[]{:S(2)}, u32[]{:S(2)}) collective-permute-start(bf16[64,512]{1,0:T(8,128)(2,1)S(1)} %get-tuple-element.38), channel_id=1, source_target_pairs={{0,12},{2,14},{4,8},{6,10},{8,4},{10,6},{12,0},{14,2},{1,13},{3,15... | collective-permute-start | bytes 196616 | tf_op jit(solution)/shard_map/ppermute | solution.py:167
  84.6 5.0 %collective-permute-start.29 = (bf16[64,512]{1,0:T(8,128)(2,1)S(1)}, bf16[64,512]{1,0:T(8,128)(2,1)S(1)}, u32[]{:S(2)}, u32[]{:S(2)}) collective-permute-start(bf16[64,512]{1,0:T(8,128)(2,1)S(1)} %get-tuple-element.37), channel_id=1, source_target_pairs={{0,4},{2,6},{4,0},{6,2},{8,12},{10,14},{12,8},{14,10},{1,5},{3,7},... | collective-permute-start | bytes 196616 | tf_op jit(solution)/shard_map/ppermute | solution.py:167
  84.6 5.2 %collective-permute-start.30 = (bf16[64,512]{1,0:T(8,128)(2,1)S(1)}, bf16[64,512]{1,0:T(8,128)(2,1)S(1)}, u32[]{:S(2)}, u32[]{:S(2)}) collective-permute-start(bf16[64,512]{1,0:T(8,128)(2,1)S(1)} %get-tuple-element.36), channel_id=1, source_target_pairs={{0,8},{2,10},{4,12},{6,14},{8,0},{10,2},{12,4},{14,6},{1,9},{3,11}... | collective-permute-start | bytes 196616 | tf_op jit(solution)/shard_map/ppermute | solution.py:167
  86.2 6.1 %collective-permute-start.31 = (bf16[64,512]{1,0:T(8,128)(2,1)S(1)}, bf16[64,512]{1,0:T(8,128)(2,1)S(1)}, u32[]{:S(2)}, u32[]{:S(2)}) collective-permute-start(bf16[64,512]{1,0:T(8,128)(2,1)S(1)} %get-tuple-element.35), channel_id=1, source_target_pairs={{0,12},{2,14},{4,8},{6,10},{8,4},{10,6},{12,0},{14,2},{1,13},{3,15... | collective-permute-start | bytes 196616 | tf_op jit(solution)/shard_map/ppermute | solution.py:167
where the time goes:
time: 93.7 us; the launch traced here: 93.5 us
  starting transfers between devices  47.5 us (51%)
  Pallas kernels  24.6 us (26%)
  waiting for transfers between devices  15.3 us (16%)
  matrix products  4.29 us (5%)
  between operations  1.14 us (1%)
    ppermute x24, starting transfers between devices, shift_long(): return lax.ppermute(x, 'hist', pairs)  37.8 us
    pallas_call x8, Pallas kernels, attend(): pl.pallas_call(functools.partial(attend_kernel, dim), grid=(width // step...  22.1 us
    ppermute x24, waiting for transfers between devices, shift_long(): return lax.ppermute(x, 'hist', pairs)  11.1 us
    ppermute x8, starting transfers between devices, swap_deep(): return lax.ppermute(x, 'hist', pairs)  9.78 us
    ppermute x8, waiting for transfers between devices, swap_deep(): return lax.ppermute(x, 'hist', pairs)  4.28 us
    dot_general x2, matrix products, per_device(): jnp.dot(hidden, w_query[0, :, c * part:(c + 1) * part], preferred_element...  3.27 us
    pallas_call x2, Pallas kernels, finish(): pl.pallas_call(functools.partial(finish_kernel, half_factor, layer, [len(...  2.38 us
  transfers between devices with their start and end apart: 32, of which 11 were waited for; matrix products, arithmetic and copies ran while one was open for 3% of the time, Pallas kernels for 24%

commit v1 on v0

--- a/solution.py
+++ b/solution.py
@@ -12,7 +12,7 @@
 CHUNKS = 2
 ROW_TILE = 256
 HIST_TILE = 512
-STEP_HEADS = 2
+STEP_HEADS = 4
 LIMITS_COST = 20
 ATTEND_VMEM = 16 * 2**20
 FINISH_VMEM = 16 * 2**20
@@ -60,7 +60,8 @@
         head = slice(c, c + dim)
         for r in range(0, rows, tile_rows):
             q = q_ref[r : r + tile_rows, head]
-            lim = lim_ref[r : r + tile_rows, :1]
+            lim = lim_ref[r : r + tile_rows, :]
+            lim = jnp.concatenate([lim] * (tile_hist // lim.shape[1]), axis=1)
 
             def score(j):
                 k = k_ref[0, 0, j : j + tile_hist, head]
@@ -196,9 +197,9 @@
         near, far = [], []
         for c in range(CHUNKS):
             q = queries[c]
-            blocks = [q] + [
-                shift_long(q, s if paired else -s) for s in range(1, long)
-            ]
+            blocks = [q]
+            for s in range(1, long):
+                blocks.append(shift_long(q, s if paired else -s))
             near.append(jnp.concatenate(blocks))
             if deep > 1:
                 far.append(swap_deep(near[c]))

time: 93.7 us -> 93.2 us (level)
  Pallas kernels: 24.6 us -> 20.6 us
  starting transfers between devices: 47.5 us -> 49.5 us
  waiting for transfers between devices: 15.3 us -> 16.9 us
    pallas_call x8, Pallas kernels: 22.1 us -> 17.9 us  [attend(): pl.pallas_call(functools.partial(attend_kernel, dim), grid=(width // step...]
    ppermute x8, starting transfers between devices: 9.78 us -> 11.9 us  [swap_deep(): return lax.ppermute(x, 'hist', pairs)]
  transfers between devices with their start and end apart: 32 -> 32, of which waited for: 11 -> 12; matrix products, arithmetic and copies ran while one was open for 3% -> 3% of each run, Pallas kernels for 24% -> 19%
where the time goes in v1:
time: 93.2 us; the launch traced here: 93 us
  starting transfers between devices  49.5 us (53%)
  Pallas kernels  20.6 us (22%)
  waiting for transfers between devices  16.9 us (18%)
  matrix products  4.29 us (5%)
  between operations  1.12 us (1%)
    ppermute x24, starting transfers between devices, shift_long(): return lax.ppermute(x, 'hist', pairs)  37.6 us
    pallas_call x8, Pallas kernels, attend(): pl.pallas_call(functools.partial(attend_kernel, dim), grid=(width // step...  17.9 us
    ppermute x8, starting transfers between devices, swap_deep(): return lax.ppermute(x, 'hist', pairs)  11.9 us
    ppermute x24, waiting for transfers between devices, shift_long(): return lax.ppermute(x, 'hist', pairs)  11.8 us
    ppermute x8, waiting for transfers between devices, swap_deep(): return lax.ppermute(x, 'hist', pairs)  5.08 us
    dot_general x2, matrix products, per_device(): jnp.dot(hidden, w_query[0, :, c * part:(c + 1) * part], preferred_element...  3.27 us
    pallas_call x2, Pallas kernels, finish(): pl.pallas_call(functools.partial(finish_kernel, half_factor, layer, [len(...  2.55 us
  transfers between devices with their start and end apart: 32, of which 12 were waited for; matrix products, arithmetic and copies ran while one was open for 3% of the time, Pallas kernels for 19%

profile of v1, /device:TPU:0, one launch (start us, length us, event | category | flops | bytes accessed | tf_op | source)
XLA Modules:
  0.0 93.0 jit_solution(1881825049986375254)
XLA Ops:
  0.0 1.6 %multiply_convert_fusion.1 = bf16[64,512]{1,0:T(8,128)(2,1)S(1)} fusion(bf16[2,1024,1024]{2,1,0:T(8,128)(2,1)} %query_w_ref.3, bf16[1,64,1024]{2,1,0:T(8,128)(2,1)} %param.9), kind=kOutput, calls=%fused_computation.21 | convolution fusion | flops 67305472 | bytes 1245184 | tf_op jit(solution)/shard_map/dot_general | solution.py:186
  1.6 5.1 %collective-permute-start.2 = (bf16[64,512]{1,0:T(8,128)(2,1)S(1)}, bf16[64,512]{1,0:T(8,128)(2,1)S(1)}, u32[]{:S(2)}, u32[]{:S(2)}) collective-permute-start(bf16[64,512]{1,0:T(8,128)(2,1)S(1)} %multiply_convert_fusion.1), channel_id=1, source_target_pairs={{0,12},{2,14},{4,8},{6,10},{8,4},{10,6},{12,0},{14,2},{1,13},{3,15... | collective-permute-start | bytes 196616 | tf_op jit(solution)/shard_map/ppermute | solution.py:168
  6.8 0.6 collective-permute-start
  7.4 1.6 %multiply_convert_fusion = bf16[64,512]{1,0:T(8,128)(2,1)S(1)} fusion(bf16[2,1024,1024]{2,1,0:T(8,128)(2,1)} %query_w_ref.3, bf16[1,64,1024]{2,1,0:T(8,128)(2,1)} %param.9), kind=kOutput, calls=%fused_computation.20 | convolution fusion | flops 67305472 | bytes 1245184 | tf_op jit(solution)/shard_map/dot_general | solution.py:186
  9.1 3.8 %collective-permute-start.10 = (bf16[64,512]{1,0:T(8,128)(2,1)S(1)}, bf16[64,512]{1,0:T(8,128)(2,1)S(1)}, u32[]{:S(2)}, u32[]{:S(2)}) collective-permute-start(bf16[64,512]{1,0:T(8,128)(2,1)S(1)} %multiply_convert_fusion), channel_id=1, source_target_pairs={{0,12},{2,14},{4,8},{6,10},{8,4},{10,6},{12,0},{14,2},{1,13},{3,15... | collective-permute-start | bytes 196616 | tf_op jit(solution)/shard_map/ppermute | solution.py:168
  13.5 0.7 collective-permute-start.8
  14.3 0.0 slice-start.2
  14.3 0.0 slice-start.1
  14.3 0.0 slice-start.3
  14.3 1.7 %collective-permute-start.3 = (bf16[256,512]{1,0:T(8,128)(2,1)S(1)}, bf16[256,512]{1,0:T(8,128)(2,1)S(1)}, u32[]{:S(2)}, u32[]{:S(2)}) collective-permute-start(bf16[256,512]{1,0:T(8,128)(2,1)S(1)} %pad_maximum_fusion.q_ref), channel_id=1, source_target_pairs={{0,2},{2,0},{4,6},{6,4},{8,10},{10,8},{12,14},{14,12},{1,3},{3,1},... | collective-permute-start | bytes 786440 | tf_op jit(solution)/shard_map/ppermute | solution.py:172
  16.1 0.2 shard_map.91
  16.2 1.9 %collective-permute-done.9 = bf16[64,512]{1,0:T(8,128)(2,1)S(1)} collective-permute-done((bf16[64,512]{1,0:T(8,128)(2,1)S(1)}, bf16[64,512]{1,0:T(8,128)(2,1)S(1)}, u32[]{:S(2)}, u32[]{:S(2)}) %collective-permute-start.9) | collective-permute-done | bytes 65568 | tf_op jit(solution)/shard_map/ppermute | solution.py:168
  18.2 0.6 collective-permute-done.8
  18.8 1.6 %collective-permute-start.11 = (bf16[256,512]{1,0:T(8,128)(2,1)S(1)}, bf16[256,512]{1,0:T(8,128)(2,1)S(1)}, u32[]{:S(2)}, u32[]{:S(2)}) collective-permute-start(bf16[256,512]{1,0:T(8,128)(2,1)S(1)} %pad_maximum_fusion.1.q_ref), channel_id=1, source_target_pairs={{0,2},{2,0},{4,6},{6,4},{8,10},{10,8},{12,14},{14,12},{1,3},{3,1},... | collective-permute-start | bytes 786440 | tf_op jit(solution)/shard_map/ppermute | solution.py:172
  20.4 2.2 %shard_map.92 = f32[256,512]{1,0:T(8,128)S(1)} custom-call(bf16[256,512]{1,0:T(8,128)(2,1)S(1)} %pad_maximum_fusion.q_ref, s32[256,128]{1,0:T(8,128)S(1)} %get-tuple-element.16.lim_ref, bf16[2,1,1536,1024]{3,2,1,0:T(8,128)(2,1)S(1)} %bitcast.30, bf16[2,1,1536,1024]{3,2,1,0:T(8,128)(2,1)S(1)} %bitcast.32), custom_call_target="tpu_custom_call" | custom-call | flops 805306368 | bytes 3670016 | tf_op jit(solution)/shard_map/pallas_call | solution.py:92
  22.7 0.0 copy-start.5
  22.7 2.2 %shard_map.93 = bf16[256,512]{1,0:T(8,128)(2,1)S(1)} custom-call(bf16[256,512]{1,0:T(8,128)(2,1)S(1)} %collective-permute-done.3.q_ref, s32[256,128]{1,0:T(8,128)S(1)} %get-tuple-element.18.lim_ref, bf16[2,1,1536,1024]{3,2,1,0:T(8,128)(2,1)S(1)} %bitcast.30, bf16[2,1,1536,1024]{3,2,1,0:T(8,128)(2,1)S(1)} %bitcast.32), custom_call_target="tpu_custom_call" | custom-call | flops 805306368 | bytes 3670016 | tf_op jit(solution)/shard_map/pallas_call | solution.py:92
  24.9 0.8 collective-permute-start.4
  25.7 0.5 divide_multiply_fusion.1.gate_ref
  26.2 2.2 %shard_map.94 = f32[256,512]{1,0:T(8,128)S(1)} custom-call(bf16[256,512]{1,0:T(8,128)(2,1)S(1)} %pad_maximum_fusion.1.q_ref, s32[256,128]{1,0:T(8,128)S(1)} %get-tuple-element.16.lim_ref, bf16[2,1,1536,1024]{3,2,1,0:T(8,128)(2,1)S(1)} %bitcast.30, bf16[2,1,1536,1024]{3,2,1,0:T(8,128)(2,1)S(1)} %bitcast.32), custom_call_target="tpu_custom_call" | custom-call | flops 805306368 | bytes 3670016 | tf_op jit(solution)/shard_map/pallas_call | solution.py:92
  28.5 0.0 copy-start.4
  28.5 2.2 %shard_map.95 = bf16[256,512]{1,0:T(8,128)(2,1)S(1)} custom-call(bf16[256,512]{1,0:T(8,128)(2,1)S(1)} %collective-permute-done.11.q_ref, s32[256,128]{1,0:T(8,128)S(1)} %get-tuple-element.18.lim_ref, bf16[2,1,1536,1024]{3,2,1,0:T(8,128)(2,1)S(1)} %bitcast.30, bf16[2,1,1536,1024]{3,2,1,0:T(8,128)(2,1)S(1)} %bitcast.32), custom_call_target="tpu_custom_call" | custom-call | flops 805306368 | bytes 3670016 | tf_op jit(solution)/shard_map/pallas_call | solution.py:92
  30.8 1.4 %collective-permute-start.12 = (bf16[256,512]{1,0:T(8,128)(2,1)S(1)}, bf16[256,512]{1,0:T(8,128)(2,1)S(1)}, u32[]{:S(2)}, u32[]{:S(2)}) collective-permute-start(bf16[256,512]{1,0:T(8,128)(2,1)S(1)} %shard_map.95), channel_id=1, source_target_pairs={{0,2},{2,0},{4,6},{6,4},{8,10},{10,8},{12,14},{14,12},{1,3},{3,1},... | collective-permute-start | bytes 786440 | tf_op jit(solution)/shard_map/ppermute | solution.py:172
  32.2 1.0 %collective-permute-done.4 = bf16[256,512]{1,0:T(8,128)(2,1)S(1)} collective-permute-done((bf16[256,512]{1,0:T(8,128)(2,1)S(1)}, bf16[256,512]{1,0:T(8,128)(2,1)S(1)}, u32[]{:S(2)}, u32[]{:S(2)}) %collective-permute-start.4) | collective-permute-done | bytes 262176 | tf_op jit(solution)/shard_map/ppermute | solution.py:172
  33.1 0.1 fusion.26
  33.2 2.0 %collective-permute-start.5 = (bf16[64,512]{1,0:T(8,128)(2,1)S(1)}, bf16[64,512]{1,0:T(8,128)(2,1)S(1)}, u32[]{:S(2)}, u32[]{:S(2)}) collective-permute-start(bf16[64,512]{1,0:T(8,128)(2,1)S(1)} %get-tuple-element.46), channel_id=1, source_target_pairs={{0,4},{2,6},{4,0},{6,2},{8,12},{10,14},{12,8},{14,10},{1,5},{3,7},... | collective-permute-start | bytes 196616 | tf_op jit(solution)/shard_map/ppermute | solution.py:168
  35.3 2.6 %collective-permute-start.6 = (bf16[64,512]{1,0:T(8,128)(2,1)S(1)}, bf16[64,512]{1,0:T(8,128)(2,1)S(1)}, u32[]{:S(2)}, u32[]{:S(2)}) collective-permute-start(bf16[64,512]{1,0:T(8,128)(2,1)S(1)} %get-tuple-element.45), channel_id=1, source_target_pairs={{0,8},{2,10},{4,12},{6,14},{8,0},{10,2},{12,4},{14,6},{1,9},{3,11}... | collective-permute-start | bytes 196616 | tf_op jit(solution)/shard_map/ppermute | solution.py:168
  37.8 0.1 collective-permute-done.12
  37.9 0.1 fusion.25
  38.0 2.5 %collective-permute-start.13 = (bf16[64,512]{1,0:T(8,128)(2,1)S(1)}, bf16[64,512]{1,0:T(8,128)(2,1)S(1)}, u32[]{:S(2)}, u32[]{:S(2)}) collective-permute-start(bf16[64,512]{1,0:T(8,128)(2,1)S(1)} %get-tuple-element.43), channel_id=1, source_target_pairs={{0,4},{2,6},{4,0},{6,2},{8,12},{10,14},{12,8},{14,10},{1,5},{3,7},... | collective-permute-start | bytes 196616 | tf_op jit(solution)/shard_map/ppermute | solution.py:168
  40.5 2.2 %collective-permute-start.14 = (bf16[64,512]{1,0:T(8,128)(2,1)S(1)}, bf16[64,512]{1,0:T(8,128)(2,1)S(1)}, u32[]{:S(2)}, u32[]{:S(2)}) collective-permute-start(bf16[64,512]{1,0:T(8,128)(2,1)S(1)} %get-tuple-element.42), channel_id=1, source_target_pairs={{0,8},{2,10},{4,12},{6,14},{8,0},{10,2},{12,4},{14,6},{1,9},{3,11}... | collective-permute-start | bytes 196616 | tf_op jit(solution)/shard_map/ppermute | solution.py:168
  42.7 0.3 collective-permute-start.15
  43.0 1.5 %collective-permute-done.7.refs_3_ = bf16[64,512]{1,0:T(8,128)(2,1)S(1)} collective-permute-done((bf16[64,512]{1,0:T(8,128)(2,1)S(1)}, bf16[64,512]{1,0:T(8,128)(2,1)S(1)}, u32[]{:S(2)}, u32[]{:S(2)}) %collective-permute-start.7) | collective-permute-done | bytes 65568 | tf_op jit(solution)/shard_map/ppermute | solution.py:168
  44.5 0.1 collective-permute-done.13.refs_5_
  44.6 2.1 %collective-permute-done.14.refs_6_ = bf16[64,512]{1,0:T(8,128)(2,1)S(1)} collective-permute-done((bf16[64,512]{1,0:T(8,128)(2,1)S(1)}, bf16[64,512]{1,0:T(8,128)(2,1)S(1)}, u32[]{:S(2)}, u32[]{:S(2)}) %collective-permute-start.14) | collective-permute-done | bytes 65568 | tf_op jit(solution)/shard_map/ppermute | solution.py:168
  46.7 2.0 %collective-permute-done.15.refs_7_ = bf16[64,512]{1,0:T(8,128)(2,1)S(1)} collective-permute-done((bf16[64,512]{1,0:T(8,128)(2,1)S(1)}, bf16[64,512]{1,0:T(8,128)(2,1)S(1)}, u32[]{:S(2)}, u32[]{:S(2)}) %collective-permute-start.15) | collective-permute-done | bytes 65568 | tf_op jit(solution)/shard_map/ppermute | solution.py:168
  48.7 1.2 %shard_map.96 = (bf16[64,1024]{1,0:T(8,128)(2,1)S(1)}, bf16[64,512]{1,0:T(8,128)(2,1)S(1)}, bf16[64,512]{1,0:T(8,128)(2,1)S(1)}) custom-call(bf16[64,1024]{1,0:T(8,128)(2,1)S(1)} %bitcast.33, f32[64,1024]{1,0:T(8,128)S(1)} %divide_multiply_fusion.1.gate_ref, f32[1,1024]{1,0:T(1,128)S(1)} %get-tuple-element.48.gain_ref, bf16[2,1024,1024]{2,1,0:T(8,128)(2,1)S(1)} %copy-done, ...), custom_call_target="tpu_custom_call" | custom-call | flops 268435456 | bytes 4194304 | tf_op jit(solution)/shard_map/pallas_call | solution.py:146
  50.0 0.1 collective-permute-start.16
  50.1 1.7 %collective-permute-start.17 = (bf16[64,512]{1,0:T(8,128)(2,1)S(1)}, bf16[64,512]{1,0:T(8,128)(2,1)S(1)}, u32[]{:S(2)}, u32[]{:S(2)}) collective-permute-start(bf16[64,512]{1,0:T(8,128)(2,1)S(1)} %get-tuple-element.22), channel_id=1, source_target_pairs={{0,8},{2,10},{4,12},{6,14},{8,0},{10,2},{12,4},{14,6},{1,9},{3,11}... | collective-permute-start | bytes 196616 | tf_op jit(solution)/shard_map/ppermute | solution.py:168
  51.7 2.7 %collective-permute-start.18 = (bf16[64,512]{1,0:T(8,128)(2,1)S(1)}, bf16[64,512]{1,0:T(8,128)(2,1)S(1)}, u32[]{:S(2)}, u32[]{:S(2)}) collective-permute-start(bf16[64,512]{1,0:T(8,128)(2,1)S(1)} %get-tuple-element.22), channel_id=1, source_target_pairs={{0,12},{2,14},{4,8},{6,10},{8,4},{10,6},{12,0},{14,2},{1,13},{3,15... | collective-permute-start | bytes 196616 | tf_op jit(solution)/shard_map/ppermute | solution.py:168
  54.4 1.7 %collective-permute-start.25 = (bf16[64,512]{1,0:T(8,128)(2,1)S(1)}, bf16[64,512]{1,0:T(8,128)(2,1)S(1)}, u32[]{:S(2)}, u32[]{:S(2)}) collective-permute-start(bf16[64,512]{1,0:T(8,128)(2,1)S(1)} %get-tuple-element.24), channel_id=1, source_target_pairs={{0,8},{2,10},{4,12},{6,14},{8,0},{10,2},{12,4},{14,6},{1,9},{3,11}... | collective-permute-start | bytes 196616 | tf_op jit(solution)/shard_map/ppermute | solution.py:168
  56.1 2.8 %collective-permute-start.26 = (bf16[64,512]{1,0:T(8,128)(2,1)S(1)}, bf16[64,512]{1,0:T(8,128)(2,1)S(1)}, u32[]{:S(2)}, u32[]{:S(2)}) collective-permute-start(bf16[64,512]{1,0:T(8,128)(2,1)S(1)} %get-tuple-element.24), channel_id=1, source_target_pairs={{0,12},{2,14},{4,8},{6,10},{8,4},{10,6},{12,0},{14,2},{1,13},{3,15... | collective-permute-start | bytes 196616 | tf_op jit(solution)/shard_map/ppermute | solution.py:168
  59.0 2.1 %collective-permute-start.19 = (bf16[256,512]{1,0:T(8,128)(2,1)S(1)}, bf16[256,512]{1,0:T(8,128)(2,1)S(1)}, u32[]{:S(2)}, u32[]{:S(2)}) collective-permute-start(bf16[256,512]{1,0:T(8,128)(2,1)S(1)} %constant_dynamic-update-slice_fusion.q_ref), channel_id=1, source_target_pairs={{0,2},{2,0},{4,6},{6,4},{8,10},{10,8},{12,14},{14,12},{1,3},{3,1},... | collective-permute-start | bytes 786440 | tf_op jit(solution)/shard_map/ppermute | solution.py:172
  61.1 2.2 %shard_map.97 = f32[256,512]{1,0:T(8,128)S(1)} custom-call(bf16[256,512]{1,0:T(8,128)(2,1)S(1)} %constant_dynamic-update-slice_fusion.q_ref, s32[256,128]{1,0:T(8,128)S(1)} %get-tuple-element.16.lim_ref, bf16[2,1,1536,1024]{3,2,1,0:T(8,128)(2,1)S(1)} %bitcast.30, bf16[2,1,1536,1024]{3,2,1,0:T(8,128)(2,1)S(1)} %bitcast.32), custom_call_target="tpu_custom_call" | custom-call | flops 805306368 | bytes 3670016 | tf_op jit(solution)/shard_map/pallas_call | solution.py:92
  63.3 1.3 %collective-permute-start.27 = (bf16[256,512]{1,0:T(8,128)(2,1)S(1)}, bf16[256,512]{1,0:T(8,128)(2,1)S(1)}, u32[]{:S(2)}, u32[]{:S(2)}) collective-permute-start(bf16[256,512]{1,0:T(8,128)(2,1)S(1)} %constant_dynamic-update-slice_fusion.4.q_ref), channel_id=1, source_target_pairs={{0,2},{2,0},{4,6},{6,4},{8,10},{10,8},{12,14},{14,12},{1,3},{3,1},... | collective-permute-start | bytes 786440 | tf_op jit(solution)/shard_map/ppermute | solution.py:172
  64.6 3.3 %collective-permute-done.19.q_ref = bf16[256,512]{1,0:T(8,128)(2,1)S(1)} collective-permute-done((bf16[256,512]{1,0:T(8,128)(2,1)S(1)}, bf16[256,512]{1,0:T(8,128)(2,1)S(1)}, u32[]{:S(2)}, u32[]{:S(2)}) %collective-permute-start.19) | collective-permute-done | bytes 262176 | tf_op jit(solution)/shard_map/ppermute | solution.py:172
  67.9 2.2 %shard_map.98 = bf16[256,512]{1,0:T(8,128)(2,1)S(1)} custom-call(bf16[256,512]{1,0:T(8,128)(2,1)S(1)} %collective-permute-done.19.q_ref, s32[256,128]{1,0:T(8,128)S(1)} %get-tuple-element.18.lim_ref, bf16[2,1,1536,1024]{3,2,1,0:T(8,128)(2,1)S(1)} %bitcast.30, bf16[2,1,1536,1024]{3,2,1,0:T(8,128)(2,1)S(1)} %bitcast.32), custom_call_target="tpu_custom_call" | custom-call | flops 805306368 | bytes 3670016 | tf_op jit(solution)/shard_map/pallas_call | solution.py:92
  70.1 2.0 %collective-permute-start.20 = (bf16[256,512]{1,0:T(8,128)(2,1)S(1)}, bf16[256,512]{1,0:T(8,128)(2,1)S(1)}, u32[]{:S(2)}, u32[]{:S(2)}) collective-permute-start(bf16[256,512]{1,0:T(8,128)(2,1)S(1)} %shard_map.98), channel_id=1, source_target_pairs={{0,2},{2,0},{4,6},{6,4},{8,10},{10,8},{12,14},{14,12},{1,3},{3,1},... | collective-permute-start | bytes 786440 | tf_op jit(solution)/shard_map/ppermute | solution.py:172
  72.2 2.2 %shard_map.99 = f32[256,512]{1,0:T(8,128)S(1)} custom-call(bf16[256,512]{1,0:T(8,128)(2,1)S(1)} %constant_dynamic-update-slice_fusion.4.q_ref, s32[256,128]{1,0:T(8,128)S(1)} %get-tuple-element.16.lim_ref, bf16[2,1,1536,1024]{3,2,1,0:T(8,128)(2,1)S(1)} %bitcast.30, bf16[2,1,1536,1024]{3,2,1,0:T(8,128)(2,1)S(1)} %bitcast.32), custom_call_target="tpu_custom_call" | custom-call | flops 805306368 | bytes 3670016 | tf_op jit(solution)/shard_map/pallas_call | solution.py:92
  74.4 2.2 %shard_map.100 = bf16[256,512]{1,0:T(8,128)(2,1)S(1)} custom-call(bf16[256,512]{1,0:T(8,128)(2,1)S(1)} %collective-permute-done.27.q_ref, s32[256,128]{1,0:T(8,128)S(1)} %get-tuple-element.18.lim_ref, bf16[2,1,1536,1024]{3,2,1,0:T(8,128)(2,1)S(1)} %bitcast.30, bf16[2,1,1536,1024]{3,2,1,0:T(8,128)(2,1)S(1)} %bitcast.32), custom_call_target="tpu_custom_call" | custom-call | flops 805306368 | bytes 3670016 | tf_op jit(solution)/shard_map/pallas_call | solution.py:92
  76.7 1.1 %collective-permute-start.28 = (bf16[256,512]{1,0:T(8,128)(2,1)S(1)}, bf16[256,512]{1,0:T(8,128)(2,1)S(1)}, u32[]{:S(2)}, u32[]{:S(2)}) collective-permute-start(bf16[256,512]{1,0:T(8,128)(2,1)S(1)} %shard_map.100), channel_id=1, source_target_pairs={{0,2},{2,0},{4,6},{6,4},{8,10},{10,8},{12,14},{14,12},{1,3},{3,1},... | collective-permute-start | bytes 786440 | tf_op jit(solution)/shard_map/ppermute | solution.py:172
  77.8 0.1 fusion.24
  77.9 1.3 %collective-permute-start.21 = (bf16[64,512]{1,0:T(8,128)(2,1)S(1)}, bf16[64,512]{1,0:T(8,128)(2,1)S(1)}, u32[]{:S(2)}, u32[]{:S(2)}) collective-permute-start(bf16[64,512]{1,0:T(8,128)(2,1)S(1)} %get-tuple-element.40), channel_id=1, source_target_pairs={{0,4},{2,6},{4,0},{6,2},{8,12},{10,14},{12,8},{14,10},{1,5},{3,7},... | collective-permute-start | bytes 196616 | tf_op jit(solution)/shard_map/ppermute | solution.py:168
  79.2 1.1 %collective-permute-start.22 = (bf16[64,512]{1,0:T(8,128)(2,1)S(1)}, bf16[64,512]{1,0:T(8,128)(2,1)S(1)}, u32[]{:S(2)}, u32[]{:S(2)}) collective-permute-start(bf16[64,512]{1,0:T(8,128)(2,1)S(1)} %get-tuple-element.39), channel_id=1, source_target_pairs={{0,8},{2,10},{4,12},{6,14},{8,0},{10,2},{12,4},{14,6},{1,9},{3,11}... | collective-permute-start | bytes 196616 | tf_op jit(solution)/shard_map/ppermute | solution.py:168
  80.3 2.1 %collective-permute-start.23 = (bf16[64,512]{1,0:T(8,128)(2,1)S(1)}, bf16[64,512]{1,0:T(8,128)(2,1)S(1)}, u32[]{:S(2)}, u32[]{:S(2)}) collective-permute-start(bf16[64,512]{1,0:T(8,128)(2,1)S(1)} %get-tuple-element.38), channel_id=1, source_target_pairs={{0,12},{2,14},{4,8},{6,10},{8,4},{10,6},{12,0},{14,2},{1,13},{3,15... | collective-permute-start | bytes 196616 | tf_op jit(solution)/shard_map/ppermute | solution.py:168
  82.3 0.8 collective-permute-done.28
  83.1 0.1 fusion.23
  83.2 1.2 %collective-permute-start.29 = (bf16[64,512]{1,0:T(8,128)(2,1)S(1)}, bf16[64,512]{1,0:T(8,128)(2,1)S(1)}, u32[]{:S(2)}, u32[]{:S(2)}) collective-permute-start(bf16[64,512]{1,0:T(8,128)(2,1)S(1)} %get-tuple-element.37), channel_id=1, source_target_pairs={{0,4},{2,6},{4,0},{6,2},{8,12},{10,14},{12,8},{14,10},{1,5},{3,7},... | collective-permute-start | bytes 196616 | tf_op jit(solution)/shard_map/ppermute | solution.py:168
  84.4 1.2 %collective-permute-start.30 = (bf16[64,512]{1,0:T(8,128)(2,1)S(1)}, bf16[64,512]{1,0:T(8,128)(2,1)S(1)}, u32[]{:S(2)}, u32[]{:S(2)}) collective-permute-start(bf16[64,512]{1,0:T(8,128)(2,1)S(1)} %get-tuple-element.36), channel_id=1, source_target_pairs={{0,8},{2,10},{4,12},{6,14},{8,0},{10,2},{12,4},{14,6},{1,9},{3,11}... | collective-permute-start | bytes 196616 | tf_op jit(solution)/shard_map/ppermute | solution.py:168
  85.6 2.1 %collective-permute-start.31 = (bf16[64,512]{1,0:T(8,128)(2,1)S(1)}, bf16[64,512]{1,0:T(8,128)(2,1)S(1)}, u32[]{:S(2)}, u32[]{:S(2)}) collective-permute-start(bf16[64,512]{1,0:T(8,128)(2,1)S(1)} %get-tuple-element.35), channel_id=1, source_target_pairs={{0,12},{2,14},{4,8},{6,10},{8,4},{10,6},{12,0},{14,2},{1,13},{3,15... | collective-permute-start | bytes 196616 | tf_op jit(solution)/shard_map/ppermute | solution.py:168
  87.7 0.5 divide_multiply_fusion.gate_ref
  88.2 2.1 %collective-permute-done.30.refs_6_ = bf16[64,512]{1,0:T(8,128)(2,1)S(1)} collective-permute-done((bf16[64,512]{1,0:T(8,128)(2,1)S(1)}, bf16[64,512]{1,0:T(8,128)(2,1)S(1)}, u32[]{:S(2)}, u32[]{:S(2)}) %collective-permute-start.30) | collective-permute-done | bytes 65568 | tf_op jit(solution)/shard_map/ppermute | solution.py:168
  90.3 1.4 %collective-permute-done.31.refs_7_ = bf16[64,512]{1,0:T(8,128)(2,1)S(1)} collective-permute-done((bf16[64,512]{1,0:T(8,128)(2,1)S(1)}, bf16[64,512]{1,0:T(8,128)(2,1)S(1)}, u32[]{:S(2)}, u32[]{:S(2)}) %collective-permute-start.31) | collective-permute-done | bytes 65568 | tf_op jit(solution)/shard_map/ppermute | solution.py:168
  91.7 1.3 %shard_map.101 = bf16[64,1024]{1,0:T(8,128)(2,1)} custom-call(bf16[64,1024]{1,0:T(8,128)(2,1)S(1)} %get-tuple-element.21.hidden_ref, f32[64,1024]{1,0:T(8,128)S(1)} %divide_multiply_fusion.gate_ref, f32[1,1024]{1,0:T(1,128)S(1)} %get-tuple-element.47.gain_ref, bf16[2,1024,1024]{2,1,0:T(8,128)(2,1)S(1)} %copy-done, bf16[2,1024,1024]{2,1,0:T(8,128)(2,1)S(1)} %copy-done.1, ...), custom_call_target="tpu_custom_call" | custom-call | flops 268435456 | bytes 4194304 | tf_op jit(solution)/shard_map/pallas_call | solution.py:146
  (60 shorter events, 0.3 us)
Async XLA Ops:
  0.0 16.1 %copy-start.3 = (s32[1,512]{1,0:T(1,128)S(1)}, s32[1,512]{1,0:T(1,128)}, u32[]{:S(2)}) copy-start(s32[1,512]{1,0:T(1,128)} %cuts_ref.1) | copy-start | bytes 6148
  1.6 11.9 %collective-permute-start.2 = (bf16[64,512]{1,0:T(8,128)(2,1)S(1)}, bf16[64,512]{1,0:T(8,128)(2,1)S(1)}, u32[]{:S(2)}, u32[]{:S(2)}) collective-permute-start(bf16[64,512]{1,0:T(8,128)(2,1)S(1)} %multiply_convert_fusion.1), channel_id=1, source_target_pairs={{0,12},{2,14},{4,8},{6,10},{8,4},{10,6},{12,0},{14,2},{1,13},{3,15... | collective-permute-start | bytes 196616 | tf_op jit(solution)/shard_map/ppermute | solution.py:168
  6.8 7.5 %collective-permute-start.1 = (bf16[64,512]{1,0:T(8,128)(2,1)S(1)}, bf16[64,512]{1,0:T(8,128)(2,1)S(1)}, u32[]{:S(2)}, u32[]{:S(2)}) collective-permute-start(bf16[64,512]{1,0:T(8,128)(2,1)S(1)} %multiply_convert_fusion.1), channel_id=1, source_target_pairs={{0,8},{2,10},{4,12},{6,14},{8,0},{10,2},{12,4},{14,6},{1,9},{3,11}... | collective-permute-start | bytes 196616 | tf_op jit(solution)/shard_map/ppermute | solution.py:168
  6.8 7.5 %collective-permute-start = (bf16[64,512]{1,0:T(8,128)(2,1)S(1)}, bf16[64,512]{1,0:T(8,128)(2,1)S(1)}, u32[]{:S(2)}, u32[]{:S(2)}) collective-permute-start(bf16[64,512]{1,0:T(8,128)(2,1)S(1)} %multiply_convert_fusion.1), channel_id=1, source_target_pairs={{0,4},{2,6},{4,0},{6,2},{8,12},{10,14},{12,8},{14,10},{1,5},{3,7},... | collective-permute-start | bytes 196616 | tf_op jit(solution)/shard_map/ppermute | solution.py:168
  9.1 7.2 %collective-permute-start.10 = (bf16[64,512]{1,0:T(8,128)(2,1)S(1)}, bf16[64,512]{1,0:T(8,128)(2,1)S(1)}, u32[]{:S(2)}, u32[]{:S(2)}) collective-permute-start(bf16[64,512]{1,0:T(8,128)(2,1)S(1)} %multiply_convert_fusion), channel_id=1, source_target_pairs={{0,12},{2,14},{4,8},{6,10},{8,4},{10,6},{12,0},{14,2},{1,13},{3,15... | collective-permute-start | bytes 196616 | tf_op jit(solution)/shard_map/ppermute | solution.py:168
  12.9 5.3 %collective-permute-start.9 = (bf16[64,512]{1,0:T(8,128)(2,1)S(1)}, bf16[64,512]{1,0:T(8,128)(2,1)S(1)}, u32[]{:S(2)}, u32[]{:S(2)}) collective-permute-start(bf16[64,512]{1,0:T(8,128)(2,1)S(1)} %multiply_convert_fusion), channel_id=1, source_target_pairs={{0,8},{2,10},{4,12},{6,14},{8,0},{10,2},{12,4},{14,6},{1,9},{3,11}... | collective-permute-start | bytes 196616 | tf_op jit(solution)/shard_map/ppermute | solution.py:168
  13.5 5.2 %collective-permute-start.8 = (bf16[64,512]{1,0:T(8,128)(2,1)S(1)}, bf16[64,512]{1,0:T(8,128)(2,1)S(1)}, u32[]{:S(2)}, u32[]{:S(2)}) collective-permute-start(bf16[64,512]{1,0:T(8,128)(2,1)S(1)} %multiply_convert_fusion), channel_id=1, source_target_pairs={{0,4},{2,6},{4,0},{6,2},{8,12},{10,14},{12,8},{14,10},{1,5},{3,7},... | collective-permute-start | bytes 196616 | tf_op jit(solution)/shard_map/ppermute | solution.py:168
  14.3 6.1 %slice-start = ((s8[6291456]{0:T(1024)(128)(4,1)}), s8[4194304]{0:T(1024)(128)(4,1)S(1)}, s32[]{:S(2)}) async-start(s8[6291456]{0:T(1024)(128)(4,1)} %bitcast.29), calls=%async_computation | async-start | bytes 8388608
  14.3 6.1 %slice-start.2 = ((s8[6291456]{0:T(1024)(128)(4,1)}), s8[4194304]{0:T(1024)(128)(4,1)S(1)}, s32[]{:S(2)}) async-start(s8[6291456]{0:T(1024)(128)(4,1)} %bitcast.31), calls=%async_computation.2 | async-start | bytes 8388608
  14.3 6.1 %slice-start.1 = ((s8[6291456]{0:T(1024)(128)(4,1)}), s8[2097152]{0:T(1024)(128)(4,1)S(1)}, s32[]{:S(2)}) async-start(s8[6291456]{0:T(1024)(128)(4,1)} %bitcast.29), calls=%async_computation.1 | async-start | bytes 4194304
  14.3 6.1 %slice-start.3 = ((s8[6291456]{0:T(1024)(128)(4,1)}), s8[2097152]{0:T(1024)(128)(4,1)S(1)}, s32[]{:S(2)}) async-start(s8[6291456]{0:T(1024)(128)(4,1)} %bitcast.31), calls=%async_computation.3 | async-start | bytes 4194304
  14.3 8.3 %collective-permute-start.3 = (bf16[256,512]{1,0:T(8,128)(2,1)S(1)}, bf16[256,512]{1,0:T(8,128)(2,1)S(1)}, u32[]{:S(2)}, u32[]{:S(2)}) collective-permute-start(bf16[256,512]{1,0:T(8,128)(2,1)S(1)} %pad_maximum_fusion.q_ref), channel_id=1, source_target_pairs={{0,2},{2,0},{4,6},{6,4},{8,10},{10,8},{12,14},{14,12},{1,3},{3,1},... | collective-permute-start | bytes 786440 | tf_op jit(solution)/shard_map/ppermute | solution.py:172
  18.8 9.7 %collective-permute-start.11 = (bf16[256,512]{1,0:T(8,128)(2,1)S(1)}, bf16[256,512]{1,0:T(8,128)(2,1)S(1)}, u32[]{:S(2)}, u32[]{:S(2)}) collective-permute-start(bf16[256,512]{1,0:T(8,128)(2,1)S(1)} %pad_maximum_fusion.1.q_ref), channel_id=1, source_target_pairs={{0,2},{2,0},{4,6},{6,4},{8,10},{10,8},{12,14},{14,12},{1,3},{3,1},... | collective-permute-start | bytes 786440 | tf_op jit(solution)/shard_map/ppermute | solution.py:172
  22.7 3.0 %copy-start.2 = (bf16[1,64,1024]{2,1,0:T(8,128)(2,1)S(1)}, bf16[1,64,1024]{2,1,0:T(8,128)(2,1)}, u32[]{:S(2)}) copy-start(bf16[1,64,1024]{2,1,0:T(8,128)(2,1)} %param.9) | copy-start | bytes 393220
  22.7 3.0 %copy-start.5 = (bf16[2,1024,1024]{2,1,0:T(8,128)(2,1)S(1)}, bf16[2,1024,1024]{2,1,0:T(8,128)(2,1)}, u32[]{:S(2)}) copy-start(bf16[2,1024,1024]{2,1,0:T(8,128)(2,1)} %param.15) | copy-start | bytes 12582916
  24.9 8.2 %collective-permute-start.4 = (bf16[256,512]{1,0:T(8,128)(2,1)S(1)}, bf16[256,512]{1,0:T(8,128)(2,1)S(1)}, u32[]{:S(2)}, u32[]{:S(2)}) collective-permute-start(bf16[256,512]{1,0:T(8,128)(2,1)S(1)} %shard_map.93), channel_id=1, source_target_pairs={{0,2},{2,0},{4,6},{6,4},{8,10},{10,8},{12,14},{14,12},{1,3},{3,1},... | collective-permute-start | bytes 786440 | tf_op jit(solution)/shard_map/ppermute | solution.py:172
  28.5 14.4 %copy-start.4 = (f32[2,1024]{1,0:T(2,128)S(1)}, f32[2,1024]{1,0:T(2,128)}, u32[]{:S(2)}) copy-start(f32[2,1024]{1,0:T(2,128)} %param.17) | copy-start | bytes 24580
  28.5 20.2 %copy-start.1 = (bf16[2,1024,1024]{2,1,0:T(8,128)(2,1)S(1)}, bf16[2,1024,1024]{2,1,0:T(8,128)(2,1)}, u32[]{:S(2)}) copy-start(bf16[2,1024,1024]{2,1,0:T(8,128)(2,1)} %query_w_ref.3) | copy-start | bytes 12582916
  30.8 18.0 %copy-start = (bf16[2,1024,1024]{2,1,0:T(8,128)(2,1)S(1)}, bf16[2,1024,1024]{2,1,0:T(8,128)(2,1)}, u32[]{:S(2)}) copy-start(bf16[2,1024,1024]{2,1,0:T(8,128)(2,1)} %out_w_ref.3) | copy-start | bytes 12582916
  30.8 7.1 %collective-permute-start.12 = (bf16[256,512]{1,0:T(8,128)(2,1)S(1)}, bf16[256,512]{1,0:T(8,128)(2,1)S(1)}, u32[]{:S(2)}, u32[]{:S(2)}) collective-permute-start(bf16[256,512]{1,0:T(8,128)(2,1)S(1)} %shard_map.95), channel_id=1, source_target_pairs={{0,2},{2,0},{4,6},{6,4},{8,10},{10,8},{12,14},{14,12},{1,3},{3,1},... | collective-permute-start | bytes 786440 | tf_op jit(solution)/shard_map/ppermute | solution.py:172
  33.2 9.4 %collective-permute-start.5 = (bf16[64,512]{1,0:T(8,128)(2,1)S(1)}, bf16[64,512]{1,0:T(8,128)(2,1)S(1)}, u32[]{:S(2)}, u32[]{:S(2)}) collective-permute-start(bf16[64,512]{1,0:T(8,128)(2,1)S(1)} %get-tuple-element.46), channel_id=1, source_target_pairs={{0,4},{2,6},{4,0},{6,2},{8,12},{10,14},{12,8},{14,10},{1,5},{3,7},... | collective-permute-start | bytes 196616 | tf_op jit(solution)/shard_map/ppermute | solution.py:168
  35.3 7.7 %collective-permute-start.6 = (bf16[64,512]{1,0:T(8,128)(2,1)S(1)}, bf16[64,512]{1,0:T(8,128)(2,1)S(1)}, u32[]{:S(2)}, u32[]{:S(2)}) collective-permute-start(bf16[64,512]{1,0:T(8,128)(2,1)S(1)} %get-tuple-element.45), channel_id=1, source_target_pairs={{0,8},{2,10},{4,12},{6,14},{8,0},{10,2},{12,4},{14,6},{1,9},{3,11}... | collective-permute-start | bytes 196616 | tf_op jit(solution)/shard_map/ppermute | solution.py:168
  37.8 6.6 %collective-permute-start.7 = (bf16[64,512]{1,0:T(8,128)(2,1)S(1)}, bf16[64,512]{1,0:T(8,128)(2,1)S(1)}, u32[]{:S(2)}, u32[]{:S(2)}) collective-permute-start(bf16[64,512]{1,0:T(8,128)(2,1)S(1)} %get-tuple-element.44), channel_id=1, source_target_pairs={{0,12},{2,14},{4,8},{6,10},{8,4},{10,6},{12,0},{14,2},{1,13},{3,15... | collective-permute-start | bytes 196616 | tf_op jit(solution)/shard_map/ppermute | solution.py:168
  38.0 6.6 %collective-permute-start.13 = (bf16[64,512]{1,0:T(8,128)(2,1)S(1)}, bf16[64,512]{1,0:T(8,128)(2,1)S(1)}, u32[]{:S(2)}, u32[]{:S(2)}) collective-permute-start(bf16[64,512]{1,0:T(8,128)(2,1)S(1)} %get-tuple-element.43), channel_id=1, source_target_pairs={{0,4},{2,6},{4,0},{6,2},{8,12},{10,14},{12,8},{14,10},{1,5},{3,7},... | collective-permute-start | bytes 196616 | tf_op jit(solution)/shard_map/ppermute | solution.py:168
  40.5 6.2 %collective-permute-start.14 = (bf16[64,512]{1,0:T(8,128)(2,1)S(1)}, bf16[64,512]{1,0:T(8,128)(2,1)S(1)}, u32[]{:S(2)}, u32[]{:S(2)}) collective-permute-start(bf16[64,512]{1,0:T(8,128)(2,1)S(1)} %get-tuple-element.42), channel_id=1, source_target_pairs={{0,8},{2,10},{4,12},{6,14},{8,0},{10,2},{12,4},{14,6},{1,9},{3,11}... | collective-permute-start | bytes 196616 | tf_op jit(solution)/shard_map/ppermute | solution.py:168
  42.7 6.1 %collective-permute-start.15 = (bf16[64,512]{1,0:T(8,128)(2,1)S(1)}, bf16[64,512]{1,0:T(8,128)(2,1)S(1)}, u32[]{:S(2)}, u32[]{:S(2)}) collective-permute-start(bf16[64,512]{1,0:T(8,128)(2,1)S(1)} %get-tuple-element.41), channel_id=1, source_target_pairs={{0,12},{2,14},{4,8},{6,10},{8,4},{10,6},{12,0},{14,2},{1,13},{3,15... | collective-permute-start | bytes 196616 | tf_op jit(solution)/shard_map/ppermute | solution.py:168
  50.0 6.1 %collective-permute-start.16 = (bf16[64,512]{1,0:T(8,128)(2,1)S(1)}, bf16[64,512]{1,0:T(8,128)(2,1)S(1)}, u32[]{:S(2)}, u32[]{:S(2)}) collective-permute-start(bf16[64,512]{1,0:T(8,128)(2,1)S(1)} %get-tuple-element.22), channel_id=1, source_target_pairs={{0,4},{2,6},{4,0},{6,2},{8,12},{10,14},{12,8},{14,10},{1,5},{3,7},... | collective-permute-start | bytes 196616 | tf_op jit(solution)/shard_map/ppermute | solution.py:168
  50.1 8.8 %collective-permute-start.17 = (bf16[64,512]{1,0:T(8,128)(2,1)S(1)}, bf16[64,512]{1,0:T(8,128)(2,1)S(1)}, u32[]{:S(2)}, u32[]{:S(2)}) collective-permute-start(bf16[64,512]{1,0:T(8,128)(2,1)S(1)} %get-tuple-element.22), channel_id=1, source_target_pairs={{0,8},{2,10},{4,12},{6,14},{8,0},{10,2},{12,4},{14,6},{1,9},{3,11}... | collective-permute-start | bytes 196616 | tf_op jit(solution)/shard_map/ppermute | solution.py:168
  51.7 7.2 %collective-permute-start.18 = (bf16[64,512]{1,0:T(8,128)(2,1)S(1)}, bf16[64,512]{1,0:T(8,128)(2,1)S(1)}, u32[]{:S(2)}, u32[]{:S(2)}) collective-permute-start(bf16[64,512]{1,0:T(8,128)(2,1)S(1)} %get-tuple-element.22), channel_id=1, source_target_pairs={{0,12},{2,14},{4,8},{6,10},{8,4},{10,6},{12,0},{14,2},{1,13},{3,15... | collective-permute-start | bytes 196616 | tf_op jit(solution)/shard_map/ppermute | solution.py:168
  54.4 6.6 %collective-permute-start.24 = (bf16[64,512]{1,0:T(8,128)(2,1)S(1)}, bf16[64,512]{1,0:T(8,128)(2,1)S(1)}, u32[]{:S(2)}, u32[]{:S(2)}) collective-permute-start(bf16[64,512]{1,0:T(8,128)(2,1)S(1)} %get-tuple-element.24), channel_id=1, source_target_pairs={{0,4},{2,6},{4,0},{6,2},{8,12},{10,14},{12,8},{14,10},{1,5},{3,7},... | collective-permute-start | bytes 196616 | tf_op jit(solution)/shard_map/ppermute | solution.py:168
  54.4 6.6 %collective-permute-start.25 = (bf16[64,512]{1,0:T(8,128)(2,1)S(1)}, bf16[64,512]{1,0:T(8,128)(2,1)S(1)}, u32[]{:S(2)}, u32[]{:S(2)}) collective-permute-start(bf16[64,512]{1,0:T(8,128)(2,1)S(1)} %get-tuple-element.24), channel_id=1, source_target_pairs={{0,8},{2,10},{4,12},{6,14},{8,0},{10,2},{12,4},{14,6},{1,9},{3,11}... | collective-permute-start | bytes 196616 | tf_op jit(solution)/shard_map/ppermute | solution.py:168
  56.1 7.2 %collective-permute-start.26 = (bf16[64,512]{1,0:T(8,128)(2,1)S(1)}, bf16[64,512]{1,0:T(8,128)(2,1)S(1)}, u32[]{:S(2)}, u32[]{:S(2)}) collective-permute-start(bf16[64,512]{1,0:T(8,128)(2,1)S(1)} %get-tuple-element.24), channel_id=1, source_target_pairs={{0,12},{2,14},{4,8},{6,10},{8,4},{10,6},{12,0},{14,2},{1,13},{3,15... | collective-permute-start | bytes 196616 | tf_op jit(solution)/shard_map/ppermute | solution.py:168
  59.0 8.9 %collective-permute-start.19 = (bf16[256,512]{1,0:T(8,128)(2,1)S(1)}, bf16[256,512]{1,0:T(8,128)(2,1)S(1)}, u32[]{:S(2)}, u32[]{:S(2)}) collective-permute-start(bf16[256,512]{1,0:T(8,128)(2,1)S(1)} %constant_dynamic-update-slice_fusion.q_ref), channel_id=1, source_target_pairs={{0,2},{2,0},{4,6},{6,4},{8,10},{10,8},{12,14},{14,12},{1,3},{3,1},... | collective-permute-start | bytes 786440 | tf_op jit(solution)/shard_map/ppermute | solution.py:172
  63.3 11.1 %collective-permute-start.27 = (bf16[256,512]{1,0:T(8,128)(2,1)S(1)}, bf16[256,512]{1,0:T(8,128)(2,1)S(1)}, u32[]{:S(2)}, u32[]{:S(2)}) collective-permute-start(bf16[256,512]{1,0:T(8,128)(2,1)S(1)} %constant_dynamic-update-slice_fusion.4.q_ref), channel_id=1, source_target_pairs={{0,2},{2,0},{4,6},{6,4},{8,10},{10,8},{12,14},{14,12},{1,3},{3,1},... | collective-permute-start | bytes 786440 | tf_op jit(solution)/shard_map/ppermute | solution.py:172
  70.1 7.6 %collective-permute-start.20 = (bf16[256,512]{1,0:T(8,128)(2,1)S(1)}, bf16[256,512]{1,0:T(8,128)(2,1)S(1)}, u32[]{:S(2)}, u32[]{:S(2)}) collective-permute-start(bf16[256,512]{1,0:T(8,128)(2,1)S(1)} %shard_map.98), channel_id=1, source_target_pairs={{0,2},{2,0},{4,6},{6,4},{8,10},{10,8},{12,14},{14,12},{1,3},{3,1},... | collective-permute-start | bytes 786440 | tf_op jit(solution)/shard_map/ppermute | solution.py:172
  76.7 6.4 %collective-permute-start.28 = (bf16[256,512]{1,0:T(8,128)(2,1)S(1)}, bf16[256,512]{1,0:T(8,128)(2,1)S(1)}, u32[]{:S(2)}, u32[]{:S(2)}) collective-permute-start(bf16[256,512]{1,0:T(8,128)(2,1)S(1)} %shard_map.100), channel_id=1, source_target_pairs={{0,2},{2,0},{4,6},{6,4},{8,10},{10,8},{12,14},{14,12},{1,3},{3,1},... | collective-permute-start | bytes 786440 | tf_op jit(solution)/shard_map/ppermute | solution.py:172
  77.9 7.7 %collective-permute-start.21 = (bf16[64,512]{1,0:T(8,128)(2,1)S(1)}, bf16[64,512]{1,0:T(8,128)(2,1)S(1)}, u32[]{:S(2)}, u32[]{:S(2)}) collective-permute-start(bf16[64,512]{1,0:T(8,128)(2,1)S(1)} %get-tuple-element.40), channel_id=1, source_target_pairs={{0,4},{2,6},{4,0},{6,2},{8,12},{10,14},{12,8},{14,10},{1,5},{3,7},... | collective-permute-start | bytes 196616 | tf_op jit(solution)/shard_map/ppermute | solution.py:168
  79.2 9.0 %collective-permute-start.22 = (bf16[64,512]{1,0:T(8,128)(2,1)S(1)}, bf16[64,512]{1,0:T(8,128)(2,1)S(1)}, u32[]{:S(2)}, u32[]{:S(2)}) collective-permute-start(bf16[64,512]{1,0:T(8,128)(2,1)S(1)} %get-tuple-element.39), channel_id=1, source_target_pairs={{0,8},{2,10},{4,12},{6,14},{8,0},{10,2},{12,4},{14,6},{1,9},{3,11}... | collective-permute-start | bytes 196616 | tf_op jit(solution)/shard_map/ppermute | solution.py:168
  80.3 8.0 %collective-permute-start.23 = (bf16[64,512]{1,0:T(8,128)(2,1)S(1)}, bf16[64,512]{1,0:T(8,128)(2,1)S(1)}, u32[]{:S(2)}, u32[]{:S(2)}) collective-permute-start(bf16[64,512]{1,0:T(8,128)(2,1)S(1)} %get-tuple-element.38), channel_id=1, source_target_pairs={{0,12},{2,14},{4,8},{6,10},{8,4},{10,6},{12,0},{14,2},{1,13},{3,15... | collective-permute-start | bytes 196616 | tf_op jit(solution)/shard_map/ppermute | solution.py:168
  83.2 5.0 %collective-permute-start.29 = (bf16[64,512]{1,0:T(8,128)(2,1)S(1)}, bf16[64,512]{1,0:T(8,128)(2,1)S(1)}, u32[]{:S(2)}, u32[]{:S(2)}) collective-permute-start(bf16[64,512]{1,0:T(8,128)(2,1)S(1)} %get-tuple-element.37), channel_id=1, source_target_pairs={{0,4},{2,6},{4,0},{6,2},{8,12},{10,14},{12,8},{14,10},{1,5},{3,7},... | collective-permute-start | bytes 196616 | tf_op jit(solution)/shard_map/ppermute | solution.py:168
  84.4 5.9 %collective-permute-start.30 = (bf16[64,512]{1,0:T(8,128)(2,1)S(1)}, bf16[64,512]{1,0:T(8,128)(2,1)S(1)}, u32[]{:S(2)}, u32[]{:S(2)}) collective-permute-start(bf16[64,512]{1,0:T(8,128)(2,1)S(1)} %get-tuple-element.36), channel_id=1, source_target_pairs={{0,8},{2,10},{4,12},{6,14},{8,0},{10,2},{12,4},{14,6},{1,9},{3,11}... | collective-permute-start | bytes 196616 | tf_op jit(solution)/shard_map/ppermute | solution.py:168
  85.6 6.1 %collective-permute-start.31 = (bf16[64,512]{1,0:T(8,128)(2,1)S(1)}, bf16[64,512]{1,0:T(8,128)(2,1)S(1)}, u32[]{:S(2)}, u32[]{:S(2)}) collective-permute-start(bf16[64,512]{1,0:T(8,128)(2,1)S(1)} %get-tuple-element.35), channel_id=1, source_target_pairs={{0,12},{2,14},{4,8},{6,10},{8,4},{10,6},{12,0},{14,2},{1,13},{3,15... | collective-permute-start | bytes 196616 | tf_op jit(solution)/shard_map/ppermute | solution.py:168
